TPU v7x, 512 devices: a whole 4x4x16 slice. The times are simulated.
512 devices in a mesh: dp: 64 (over z_lo, y, core), expert: 8 (over z_hi, x).
Axes of the slice: x: 4, y: 4, z: 16 (z_hi: 2, z_lo: 8; z = z_hi * 8 + z_lo), core: 2. Of those that a mesh axis runs over, the one named last changes fastest.
Arguments:
- tokens: bfloat16 [1024, 6144], P('dp', 'expert'), may hold values from -6 to 6
- expert_ids: int32 [1024, 2], P('dp'), may hold values from 0 to 7, all different within a row; in each aligned block of 16 rows (0 to 15, 16 to 31, ...) at most 8 rows name the same one
- gate_probs: float32 [1024, 2], P('dp'), may hold values from 0.1 to 1
- w_gate: bfloat16 [8, 6144, 8192], P('expert', None, 'dp'), may hold values from -0.078125 to 0.078125
- w_up: bfloat16 [8, 6144, 8192], P('expert', None, 'dp'), may hold values from -0.078125 to 0.078125
- w_down_t: bfloat16 [8, 6144, 8192], P('expert', 'dp'), may hold values from -0.0625 to 0.0625
Outputs:
- mixed: bfloat16 [1024, 6144], P('dp', 'expert')
Inputs may be any that keep to these rules, and one draw needn't show every extreme that they name: `expert_ids`: each row names 2 different experts. Among the 16 rows of one index of dp no expert is named more than 8 times, a bound that some block reaches.
All inputs are finite; a program needn't handle non-finite values.
Results may differ from a plain program's by a relative error of at most 0.0057.
Values may be sent and summed in bfloat16 or wider, within the bound.
No kernel may reach another device: no remote copies, remote signals or barrier semaphores. Data moves between devices by JAX's collectives and lax.ppermute only.
A program may use at most 64 MiB of HBM per device.

v0:
```python
import jax
import jax.numpy as jnp
from jax import lax
from jax.sharding import PartitionSpec as P


def assignments(expert_ids, experts, capacity):
    flat = expert_ids.reshape(-1)
    onehot = (flat[:, None] == jnp.arange(experts, dtype=jnp.int32)[None, :]).astype(jnp.int32)
    earlier = jnp.cumsum(onehot, axis=0) - onehot
    position = jnp.sum(earlier * onehot, axis=1).reshape(expert_ids.shape)
    expert_hit = (
        expert_ids[:, :, None] == jnp.arange(experts, dtype=jnp.int32)[None, None, :]
    ).astype(jnp.float32)
    slot_hit = (
        position[:, :, None] == jnp.arange(capacity, dtype=jnp.int32)[None, None, :]
    ).astype(jnp.float32)
    return (expert_hit, slot_hit)


def per_device(tokens, expert_ids, gate_probs, w_gate, w_up, w_down_t):
    local_experts = w_gate.shape[0]
    expert_count = lax.axis_size("expert")
    dp_count = lax.axis_size("dp")
    experts = local_experts * expert_count
    capacity = tokens.shape[0] // 2
    expert_hit, slot_hit = assignments(expert_ids, experts, capacity)
    dispatch_map = jnp.einsum("tke,tkc->ect", expert_hit, slot_hit).astype(jnp.bfloat16)
    combine_map = jnp.einsum(
        "tk,tke,tkc->tec", gate_probs, expert_hit, slot_hit, precision=lax.Precision.HIGHEST
    )
    slots = jnp.einsum(
        "ect,td->ecd", dispatch_map, tokens, preferred_element_type=jnp.float32
    ).astype(jnp.bfloat16)
    arrived = lax.all_to_all(slots, "expert", split_axis=0, concat_axis=2, tiled=True)
    piece = lax.all_gather(arrived, "dp", axis=1, tiled=True)
    gate = jnp.einsum("erd,edf->erf", piece, w_gate, preferred_element_type=jnp.float32)
    up = jnp.einsum("erd,edf->erf", piece, w_up, preferred_element_type=jnp.float32)
    hidden = (jax.nn.silu(gate) * up).astype(jnp.bfloat16)
    partial_out = jnp.einsum(
        "erf,edf->erd",
        lax.all_gather(hidden, "dp", axis=2, tiled=True),
        w_down_t,
        preferred_element_type=jnp.float32,
    )
    results = partial_out.astype(jnp.bfloat16).reshape(
        local_experts, dp_count, capacity, w_down_t.shape[1]
    )
    results = lax.all_to_all(results, "dp", split_axis=1, concat_axis=3, tiled=True)
    results = results.reshape(local_experts, capacity, results.shape[3])
    slice_width = tokens.shape[1]
    outgoing = results.reshape(local_experts, capacity, expert_count, slice_width)
    returned = lax.all_to_all(outgoing, "expert", split_axis=2, concat_axis=0, tiled=True)
    returned = returned.reshape(experts, capacity, slice_width)
    mixed = jnp.einsum(
        "tec,ecd->td", combine_map, returned.astype(jnp.float32), precision=lax.Precision.HIGHEST
    )
    return mixed.astype(jnp.bfloat16)


def solution(mesh):
    placed = (
        P("dp", "expert"),
        P("dp", None),
        P("dp", None),
        P("expert", None, "dp"),
        P("expert", None, "dp"),
        P("expert", "dp", None),
    )
    return jax.shard_map(
        per_device, mesh=mesh, in_specs=placed, out_specs=P("dp", "expert"), check_vma=False
    )
```

profile of v0, /device:TPU:32, one launch (start us, length us, event | category | flops | bytes accessed | tf_op | source)
XLA Modules:
  0.0 365.9 jit_solution(194935779494038113)
XLA Ops:
  6.5 0.9 copy.24
  7.4 0.1 eq.46
  7.5 0.1 fusion.27
  7.6 0.2 select_reduce_fusion
  7.8 0.1 eq.50
  7.9 0.3 fusion.22
  8.2 0.1 copy.27
  8.3 0.9 convolution_convert_fusion
  9.2 33.7 %all_to_all.48 = bf16[8,8,768]{2,1,0:T(8,128)(2,1)} all-to-all(bf16[8,8,768]{2,1,0:T(8,128)(2,1)S(1)} %convolution_convert_fusion), channel_id=1, replica_groups=mesh['dp'=64,'expert'=8] {'expert'}, dimensions={0} | all-to-all | bytes 196608 | tf_op jit(solution)/shard_map/all_to_all | solution.py:35
  42.9 116.0 %all-gather.4.cloned.1.call-done = bf16[1,512,6144]{2,1,0:T(8,128)(2,1)} async-done(((bf16[1,8,6144]{2,1,0:T(8,128)(2,1)}), bf16[1,512,6144]{2,1,0:T(8,128)(2,1)}) %all-gather.4.cloned.1.call-update) | async-done | bytes 6291472 | tf_op jit(solution)/shard_map/all_gather | solution.py:36
  158.9 4.7 %fusion.2 = f32[512,128]{1,0:T(8,128)S(1)} fusion(bf16[1,512,6144]{2,1,0:T(8,128)(2,1)} %all-gather.4.cloned.1.call-done, bf16[1,6144,128]{2,1,0:T(8,128)(2,1)S(1)} %copy-done), kind=kOutput, calls=%fused_computation.2 | convolution fusion | flops 805306368 | bytes 8126464 | tf_op jit(solution)/shard_map/erd,edf->erf/dot_general | solution.py:37
  163.7 4.0 %fusion.13 = bf16[512,128]{1,0:T(8,128)(2,1)} fusion(bf16[1,6144,128]{2,1,0:T(8,128)(2,1)} %param.10, bf16[1,512,6144]{2,1,0:T(8,128)(2,1)S(1)} %copy-done.3, f32[512,128]{1,0:T(8,128)S(1)} %fusion.2), kind=kOutput, calls=%fused_computation.9 | convolution fusion | flops 805699584 | bytes 8257536 | tf_op jit(solution)/shard_map/erd,edf->erf/dot_general | solution.py:38
  167.7 133.2 %all-gather.6.cloned.1.call-done = bf16[512,8192]{1,0:T(8,128)(2,1)} async-done(((bf16[512,128]{1,0:T(8,128)(2,1)}), bf16[512,8192]{1,0:T(8,128)(2,1)}) %all-gather.6.cloned.1.call-update) | async-done | bytes 8388624 | tf_op jit(solution)/shard_map/all_gather | solution.py:42
  300.9 6.2 %fusion.18 = bf16[512,96]{0,1:T(8,128)(2,1)S(1)} fusion(bf16[512,8192]{1,0:T(8,128)(2,1)} %all-gather.6.cloned.1.call-done, bf16[1,96,8192]{2,1,0:T(8,128)(2,1)S(1)} %copy-done.1), kind=kOutput, calls=%fused_computation.10 | convolution fusion | flops 805355520 | bytes 10059776 | tf_op jit(solution)/shard_map/erf,edf->erd/dot_general | solution.py:40
  307.1 0.1 copy.28
  307.2 22.8 %all_to_all.49 = bf16[1,64,8,96]{3,2,0,1:T(8,128)(2,1)S(1)} all-to-all(bf16[1,64,8,96]{3,2,0,1:T(8,128)(2,1)S(1)} %bitcast.56), channel_id=1, replica_groups=mesh['dp'=64,'expert'=8] {'dp'}, dimensions={1} | all-to-all | bytes 196608 | tf_op jit(solution)/shard_map/all_to_all | solution.py:49
  330.1 0.1 reshape_reshape.3
  330.2 0.7 copy.31
  330.8 10.6 %all-to-all-start.2 = ((bf16[1,8,8,768]{3,1,0,2:T(8,128)(2,1)}), bf16[1,8,8,768]{3,1,0,2:T(8,128)(2,1)S(1)}, u32[]{:S(2)}, u32[]{:S(2)}) async-start(bf16[1,8,8,768]{3,1,0,2:T(8,128)(2,1)} %copy.31), calls=%async_computation.2 | async-start | bytes 196608 | tf_op jit(solution)/shard_map/all_to_all | solution.py:53
  341.4 0.1 copy.25
  341.5 0.4 fusion.26
  341.9 0.1 copy.33
  342.0 16.2 %all-to-all-done.2 = bf16[1,8,8,768]{3,1,0,2:T(8,128)(2,1)S(1)} async-done(((bf16[1,8,8,768]{3,1,0,2:T(8,128)(2,1)}), bf16[1,8,8,768]{3,1,0,2:T(8,128)(2,1)S(1)}, u32[]{:S(2)}, u32[]{:S(2)}) %all-to-all-start.2) | async-done | bytes 98336 | tf_op jit(solution)/shard_map/all_to_all | solution.py:53
  358.3 0.8 fusion.21
  (14 shorter events, 0.2 us)
Async XLA Ops:
  6.5 152.4 %copy-start = (bf16[1,6144,128]{2,1,0:T(8,128)(2,1)S(1)}, bf16[1,6144,128]{2,1,0:T(8,128)(2,1)}, u32[]{:S(2)}) copy-start(bf16[1,6144,128]{2,1,0:T(8,128)(2,1)} %param.9) | copy-start | bytes 4718596
  6.5 152.4 %all-gather.4.cloned.1.call-start = ((), (), s32[]{:S(2)}) async-start(), calls=%async_computation.3 | async-start | bytes 6389760 | tf_op jit(solution)/shard_map/all_gather | solution.py:36
  42.9 258.0 %all-gather.6.cloned.1.call-start = ((), (), s32[]{:S(2)}) async-start(), calls=%async_computation.4 | async-start | bytes 8519680 | tf_op jit(solution)/shard_map/all_gather | solution.py:42
  158.9 4.7 %copy-start.3 = (bf16[1,512,6144]{2,1,0:T(8,128)(2,1)S(1)}, bf16[1,512,6144]{2,1,0:T(8,128)(2,1)}, u32[]{:S(2)}) copy-start(bf16[1,512,6144]{2,1,0:T(8,128)(2,1)} %all-gather.4.cloned.1.call-done) | copy-start | bytes 18874372
  163.7 137.2 %copy-start.1 = (bf16[1,96,8192]{2,1,0:T(8,128)(2,1)S(1)}, bf16[1,96,8192]{2,1,0:T(8,128)(2,1)}, u32[]{:S(2)}) copy-start(bf16[1,96,8192]{2,1,0:T(8,128)(2,1)} %param.11) | copy-start | bytes 4718596
  167.7 173.7 %copy-start.2 = (f32[16,2]{0,1:T(2,128)S(1)}, f32[16,2]{0,1:T(2,128)}, u32[]{:S(2)}) copy-start(f32[16,2]{0,1:T(2,128)} %param.8) | copy-start | bytes 388
  330.8 27.4 %all-to-all-start.2 = ((bf16[1,8,8,768]{3,1,0,2:T(8,128)(2,1)}), bf16[1,8,8,768]{3,1,0,2:T(8,128)(2,1)S(1)}, u32[]{:S(2)}, u32[]{:S(2)}) async-start(bf16[1,8,8,768]{3,1,0,2:T(8,128)(2,1)} %copy.31), calls=%async_computation.2 | async-start | bytes 196608 | tf_op jit(solution)/shard_map/all_to_all | solution.py:53
Sparse Core Ops, SparseCore 0:
  43.0 115.8 all-gather.3
  167.8 133.0 all-gather.5
where the time goes:
time: 366 us
  waiting for transfers between devices  265 us (72%)
  blocking collectives  56.5 us (15%)
  matrix products  17.3 us (5%)
  between operations  13.5 us (4%)
  starting transfers between devices  10.6 us (3%)
    all_gather x1, waiting for transfers between devices, per_device(): lax.all_gather(hidden, 'dp', axis=2, tiled=True)  133 us
    all_gather x1, waiting for transfers between devices, per_device(): piece = lax.all_gather(arrived, 'dp', axis=1, tiled=True)  116 us
    all_to_all x1, blocking collectives, per_device(): lax.all_to_all(slots, 'expert', split_axis=0, concat_axis=2, tiled=True)  33.7 us
    all_to_all x1, blocking collectives, per_device(): lax.all_to_all(results, 'dp', split_axis=1, concat_axis=3, tiled=True)  22.8 us
    all_to_all x1, waiting for transfers between devices, per_device(): lax.all_to_all(outgoing, 'expert', split_axis=2, concat_axis=0, tiled=True)  16.2 us
    all_to_all x1, starting transfers between devices, per_device(): lax.all_to_all(outgoing, 'expert', split_axis=2, concat_axis=0, tiled=True)  10.6 us
  transfers between devices with their start and end apart: 3, of which 3 were waited for; matrix products, arithmetic and copies ran while one was open for 0% of the time, Pallas kernels for 0%

commit v1 on v0

v1 whole, which is shorter than its diff:
```python
import jax
import jax.numpy as jnp
from jax import lax
from jax.sharding import Mesh, PartitionSpec as P

AXES = ("zl", "y", "c", "zh", "x")
SIZES = (8, 4, 2, 2, 4)
SWAP = [(0, 1), (1, 0)]


def everyone(value, axis, count):
    return lax.all_to_all(
        jnp.broadcast_to(value[None], (count,) + value.shape), axis, 0, 0, tiled=True
    )


def slot_numbers(expert_ids, capacity):
    flat = expert_ids.reshape(-1)
    pairs = flat.shape[0]
    same = flat[:, None] == flat[None, :]
    index = jnp.arange(pairs, dtype=jnp.int32)
    earlier = index[None, :] < index[:, None]
    position = jnp.sum((same & earlier).astype(jnp.int32), axis=1)
    return (flat * capacity + position).reshape(expert_ids.shape)


def per_device(tokens, expert_ids, gate_probs, w_gate, w_up, w_down_t):
    zl, y, c, zh, x = SIZES
    block, width = tokens.shape
    capacity = block // 2
    experts = zh * x
    model = width * experts
    units = w_gate.shape[2]
    f32, bf16 = jnp.float32, jnp.bfloat16

    gate_own, up_own = w_gate[0], w_up[0]
    gate_far = lax.ppermute(gate_own, "c", SWAP)
    up_far = lax.ppermute(up_own, "c", SWAP)
    features = w_down_t.shape[1]
    down = w_down_t[0].reshape(features, zl, y, c * units).transpose(2, 0, 1, 3)
    down = lax.all_to_all(
        down.reshape(y, features, zl * c * units), "y", 0, 0, tiled=True
    ).reshape(y * features, zl * c * units)
    down_far = lax.ppermute(down, "c", SWAP)

    slot = slot_numbers(expert_ids, capacity)
    tail = jnp.pad(slot, ((0, 0), (0, 126)), constant_values=0).astype(bf16)
    seen = everyone(jnp.concatenate([tokens, tail], axis=1), ("zh", "zl"), zh * zl)
    seen = seen.reshape(zh, zl * block, width + 128)
    slot_seen = seen[0, :, width : width + 2].astype(f32).astype(jnp.int32)

    rows = zl * capacity
    wanted = (
        lax.axis_index("zh") * (x * capacity)
        + jnp.arange(x, dtype=jnp.int32)[:, None, None] * capacity
        + jnp.arange(capacity, dtype=jnp.int32)[None, None, :]
        + jnp.zeros((1, zl, 1), jnp.int32)
    ).reshape(-1)
    row_block = (jnp.arange(x * rows, dtype=jnp.int32) // capacity) % zl
    token_block = jnp.arange(zl * block, dtype=jnp.int32) // block
    hit = (slot_seen[:, 0][None, :] == wanted[:, None]) | (
        slot_seen[:, 1][None, :] == wanted[:, None]
    )
    hit = (hit & (row_block[:, None] == token_block[None, :])).astype(bf16)
    slots = jnp.concatenate(
        [
            jnp.dot(hit, seen[h, :, :width], preferred_element_type=f32)
            .astype(bf16)
            .reshape(x, rows, width)
            for h in range(zh)
        ],
        axis=1,
    )
    arrived = lax.all_to_all(slots, "x", 0, 0, tiled=True)
    piece = jnp.concatenate(
        [arrived[i, h * rows : (h + 1) * rows] for h in range(zh) for i in range(x)],
        axis=1,
    )
    piece = everyone(piece, "y", y).reshape(y * rows, model)

    def act(w1, w2):
        gate = jnp.dot(piece, w1, preferred_element_type=f32)
        up = jnp.dot(piece, w2, preferred_element_type=f32)
        return (jax.nn.silu(gate) * up).astype(bf16)

    first = lax.axis_index("c") == 0
    own, far = act(gate_own, up_own), act(gate_far, up_far)
    hidden = jnp.concatenate(
        [jnp.where(first, own, far), jnp.where(first, far, own)], axis=1
    )
    hidden = everyone(hidden, "zl", zl)
    hidden = hidden.transpose(1, 0, 2).reshape(y * rows, zl * c * units)

    def out(w):
        part = lax.dot_general(
            hidden, w, (((1,), (1,)), ((), ())), preferred_element_type=f32
        )
        return part.astype(bf16)

    own, far = out(down), out(down_far)
    part = jnp.concatenate(
        [jnp.where(first, own, far), jnp.where(first, far, own)], axis=1
    ).reshape(y, rows, width)
    part = lax.all_to_all(part, "y", 0, 0, tiled=True).astype(f32)
    result = ((part[0] + part[1]) + (part[2] + part[3])).astype(bf16)

    result = lax.all_to_all(
        result.reshape(zl, capacity, width), "zl", 0, 0, tiled=True
    )
    result = lax.all_to_all(result, ("zh", "x"), 0, 0, tiled=True)
    result = result.reshape(experts * capacity, width)

    every = jnp.arange(experts * capacity, dtype=jnp.int32)
    mixed = 0.0
    for k in range(2):
        pick = (slot[:, k][:, None] == every[None, :]).astype(bf16)
        picked = jnp.dot(pick, result, preferred_element_type=f32)
        mixed = mixed + gate_probs[:, k][:, None] * picked
    mixed = mixed.astype(bf16).reshape(block, c, y, features)
    return mixed.transpose(0, 2, 1, 3).reshape(block, width)


def solution(mesh):
    physical = Mesh(mesh.devices.reshape(SIZES), AXES)
    dp, expert = AXES[:3], AXES[3:]
    placed = (
        P(dp, expert),
        P(dp, None),
        P(dp, None),
        P(expert, None, dp),
        P(expert, None, dp),
        P(expert, dp, None),
    )
    return jax.shard_map(
        per_device,
        mesh=physical,
        in_specs=placed,
        out_specs=P(dp, expert),
        check_vma=False,
    )
```

time: 366 us -> 233 us (0.64)
  waiting for transfers between devices: 265 us -> 111 us
  starting transfers between devices: 10.6 us -> 49 us
  blocking collectives: 56.5 us -> 40.8 us
  local copies, waits for them, and re-layouts: 2.28 us -> 16.6 us
  between operations: 13.5 us -> 0.33 us
  matrix products: 17.3 us -> 13 us
    all_gather x2 -> x0, waiting for transfers between devices: 249 us -> none  [the longest x1 133 us: per_device(): lax.all_gather(hidden, 'dp', axis=2, tiled=True)]
    all_to_all x1 -> x5, waiting for transfers between devices: 16.2 us -> 111 us  [the longest x3 86.6 us: everyone(): lax.all_to_all(jnp.broadcast_to(value[None], (count,) + value.shape), axi...]
    all_to_all x1 -> x5, starting transfers between devices: 10.6 us -> 42.8 us  [the longest x3 33.8 us: everyone(): lax.all_to_all(jnp.broadcast_to(value[None], (count,) + value.shape), axi...]
    all_to_all x2 -> x3, blocking collectives: 56.5 us -> 40.8 us  [the longest x1 16.5 us: per_device(): lax.all_to_all(result.reshape(zl, capacity, width), 'zl', 0, 0, tiled=True)]
    ppermute x0 -> x3, starting transfers between devices: none -> 6.23 us  [the longest x1 2.41 us: per_device(): up_far = lax.ppermute(up_own, 'c', SWAP)]
    another operation x2, local copies, waits for them, and re-layouts: 0.79 us -> 6.7 us  [per_device(): down = w_down_t[0].reshape(features, zl, y, c * units).transpose(2, 0, 1, 3)]
    reshape x0 -> x3, local copies, waits for them, and re-layouts: none -> 4.55 us  [the longest x1 3.74 us: per_device(): down.reshape(y, features, zl * c * units)]
    dot_general x7 -> x10, matrix products: 17.3 us -> 13 us  [the longest x2 5.25 us: act(): gate = jnp.dot(piece, w1, preferred_element_type=f32)]
  transfers between devices with their start and end apart: 3 -> 8, of which waited for: 3 -> 5; matrix products, arithmetic and copies ran while one was open for 0% -> 9% of each run, Pallas kernels for 0% -> 0%
where the time goes in v1:
time: 233 us; the launch traced here: 232 us
  waiting for transfers between devices  111 us (48%)
  starting transfers between devices  49 us (21%)
  blocking collectives  40.8 us (18%)
  local copies, waits for them, and re-layouts  16.6 us (7%)
  matrix products  13 us (6%)
    all_to_all x3, waiting for transfers between devices, everyone(): lax.all_to_all(jnp.broadcast_to(value[None], (count,) + value.shape), axi...  86.6 us
    all_to_all x3, starting transfers between devices, everyone(): lax.all_to_all(jnp.broadcast_to(value[None], (count,) + value.shape), axi...  33.8 us
    all_to_all x1, blocking collectives, per_device(): lax.all_to_all(result.reshape(zl, capacity, width), 'zl', 0, 0, tiled=True)  16.5 us
    all_to_all x1, waiting for transfers between devices, per_device(): result = lax.all_to_all(result, ('zh', 'x'), 0, 0, tiled=True)  16.4 us
    all_to_all x1, blocking collectives, per_device(): arrived = lax.all_to_all(slots, 'x', 0, 0, tiled=True)  14.5 us
    all_to_all x1, blocking collectives, per_device(): part = lax.all_to_all(part, 'y', 0, 0, tiled=True).astype(f32)  9.77 us
    all_to_all x1, waiting for transfers between devices, per_device(): lax.all_to_all(down.reshape(y, features, zl * c * units), 'y', 0, 0, tile...  7.48 us
    another operation x2, local copies, waits for them, and re-layouts, per_device(): down = w_down_t[0].reshape(features, zl, y, c * units).transpose(2, 0, 1, 3)  6.7 us
  transfers between devices with their start and end apart: 8, of which 5 were waited for; matrix products, arithmetic and copies ran while one was open for 9% of the time, Pallas kernels for 0%

profile of v1, /device:TPU:32, one launch (start us, length us, event | category | flops | bytes accessed | tf_op | source)
XLA Modules:
  0.0 232.1 jit_solution(1655345399882967015)
XLA Ops:
  3.6 15.2 %all-to-all-start = ((bf16[16,16,896]{2,1,0:T(8,128)(2,1)}), bf16[16,16,896]{2,1,0:T(8,128)(2,1)S(1)}, u32[]{:S(2)}, u32[]{:S(2)}) async-start(bf16[16,16,896]{2,1,0:T(8,128)(2,1)} %broadcast_in_dim.6), calls=%async_computation | async-start | bytes 917504 | tf_op jit(solution)/shard_map/all_to_all | solution.py:12
  19.0 23.9 %all-to-all-done = bf16[16,16,896]{2,1,0:T(8,128)(2,1)S(1)} async-done(((bf16[16,16,896]{2,1,0:T(8,128)(2,1)}), bf16[16,16,896]{2,1,0:T(8,128)(2,1)S(1)}, u32[]{:S(2)}, u32[]{:S(2)}) %all-to-all-start) | async-done | bytes 458784 | tf_op jit(solution)/shard_map/all_to_all | solution.py:12
  43.8 14.5 %all_to_all.40 = bf16[4,128,768]{2,1,0:T(8,128)(2,1)S(1)} all-to-all(bf16[4,128,768]{2,1,0:T(8,128)(2,1)S(1)} %pad_maximum_fusion), channel_id=1, replica_groups=mesh['zl'=8,'y'=4,'c'=2,'zh'=2,'x'=4] {'x'}, dimensions={0} | all-to-all | bytes 1572864 | tf_op jit(solution)/shard_map/all_to_all | solution.py:74
  58.5 2.0 broadcast_in_dim.7
  60.5 4.5 %all-to-all-start.2 = ((bf16[4,64,6144]{2,1,0:T(8,128)(2,1)}), bf16[4,64,6144]{2,1,0:T(8,128)(2,1)S(1)}, u32[]{:S(2)}, u32[]{:S(2)}) async-start(bf16[4,64,6144]{2,1,0:T(8,128)(2,1)} %broadcast_in_dim.7), calls=%async_computation.2 | async-start | bytes 6291456 | tf_op jit(solution)/shard_map/all_to_all | solution.py:12
  64.9 1.9 collective-permute-start
  66.8 2.4 %collective-permute-start.1 = (bf16[6144,128]{1,0:T(8,128)(2,1)}, bf16[6144,128]{1,0:T(8,128)(2,1)}, u32[]{:S(2)}, u32[]{:S(2)}) collective-permute-start(bf16[6144,128]{1,0:T(8,128)(2,1)} %bitcast.96), channel_id=1, source_target_pairs={{0,8},{8,0},{1,9},{9,1},{2,10},{10,2},{3,11},{11,3},{4,12},{12,4},... | collective-permute-start | bytes 4718600 | tf_op jit(solution)/shard_map/ppermute | solution.py:38
  69.3 3.9 %reshape_squeeze.3 = bf16[96,8,4,256]{3,2,1,0:T(4,128)(2,1)} reshape(bf16[1,96,8192]{2,1,0:T(8,128)(2,1)} %param.11) | data formatting | bytes 3145728 | tf_op jit(solution)/shard_map/reshape;squeeze | solution.py:40
  73.1 2.9 %copy.34 = bf16[96,8,4,256]{3,1,0,2:T(8,128)(2,1)} copy(bf16[96,8,4,256]{3,2,1,0:T(4,128)(2,1)} %reshape_squeeze.3) | data formatting | bytes 3145728 | tf_op jit(solution)/shard_map/reshape;squeeze | solution.py:40
  76.0 3.7 %reshape.126 = bf16[4,96,2048]{2,1,0:T(8,128)(2,1)} reshape(bf16[4,96,8,256]{3,2,1,0:T(8,128)(2,1)} %bitcast.90) | data formatting | bytes 3145728 | tf_op jit(solution)/shard_map/reshape | solution.py:42
  79.7 19.5 %all-to-all-done.2 = bf16[4,64,6144]{2,1,0:T(8,128)(2,1)S(1)} async-done(((bf16[4,64,6144]{2,1,0:T(8,128)(2,1)}), bf16[4,64,6144]{2,1,0:T(8,128)(2,1)S(1)}, u32[]{:S(2)}, u32[]{:S(2)}) %all-to-all-start.2) | async-done | bytes 3145760 | tf_op jit(solution)/shard_map/all_to_all | solution.py:12
  99.2 4.3 %all-to-all-start.4 = ((bf16[4,96,2048]{2,1,0:T(8,128)(2,1)}), bf16[4,96,2048]{2,1,0:T(8,128)(2,1)}, u32[]{:S(2)}, u32[]{:S(2)}) async-start(bf16[4,96,2048]{2,1,0:T(8,128)(2,1)} %reshape.126), calls=%async_computation.4 | async-start | bytes 3145728 | tf_op jit(solution)/shard_map/all_to_all | solution.py:41
  103.6 2.6 %fusion.23 = f32[256,128]{0,1:T(8,128)S(1)} fusion(bf16[256,6144]{1,0:T(8,128)(2,1)S(1)} %bitcast.86, bf16[1,6144,128]{2,1,0:T(8,128)(2,1)} %param.9), kind=kOutput, calls=%fused_computation.78 | convolution fusion | flops 402653184 | bytes 4849664 | tf_op jit(solution)/shard_map/dot_general | solution.py:82
  106.2 2.7 %fusion.26 = f32[256,128]{0,1:T(8,128)S(1)} fusion(bf16[256,6144]{1,0:T(8,128)(2,1)S(1)} %bitcast.87, bf16[6144,128]{1,0:T(8,128)(2,1)} %collective-permute-done), kind=kOutput, calls=%fused_computation.81 | convolution fusion | flops 402653184 | bytes 4849664 | tf_op jit(solution)/shard_map/dot_general | solution.py:82
  110.1 2.6 %broadcast_select_fusion.3 = (bf16[256,128]{0,1:T(8,128)(2,1)S(1)}, bf16[256,128]{0,1:T(8,128)(2,1)S(1)}) fusion(bf16[256,128]{0,1:T(8,128)(2,1)S(1)} %fusion, pred[]{:T(512)S(6)} %eq.101, f32[256,128]{0,1:T(8,128)S(1)} %fusion.26, bf16[256,6144]{1,0:T(8,128)(2,1)S(1)} %bitcast.89, bf16[6144,128]{1,0:T(8,128)(2,1)} %collective-permute-done.1), kind=kOutput, calls=%fused_computation.47 | convolution fusion | flops 402882560 | bytes 5046273 | tf_op jit(solution)/shard_map/dot_general | solution.py:83
  112.7 7.5 %all-to-all-done.4 = bf16[4,96,2048]{2,1,0:T(8,128)(2,1)} async-done(((bf16[4,96,2048]{2,1,0:T(8,128)(2,1)}), bf16[4,96,2048]{2,1,0:T(8,128)(2,1)}, u32[]{:S(2)}, u32[]{:S(2)}) %all-to-all-start.4) | async-done | bytes 1572896 | tf_op jit(solution)/shard_map/all_to_all | solution.py:41
  121.2 14.1 %all-to-all-start.3 = ((bf16[8,256,256]{1,2,0:T(8,128)(2,1)}), bf16[8,256,256]{1,2,0:T(8,128)(2,1)S(1)}, u32[]{:S(2)}, u32[]{:S(2)}) async-start(bf16[8,256,256]{1,2,0:T(8,128)(2,1)} %broadcast_in_dim.8), calls=%async_computation.3 | async-start | bytes 2097152 | tf_op jit(solution)/shard_map/all_to_all | solution.py:12
  135.3 1.9 collective-permute-start.2
  137.3 43.2 %all-to-all-done.3 = bf16[8,256,256]{1,2,0:T(8,128)(2,1)S(1)} async-done(((bf16[8,256,256]{1,2,0:T(8,128)(2,1)}), bf16[8,256,256]{1,2,0:T(8,128)(2,1)S(1)}, u32[]{:S(2)}, u32[]{:S(2)}) %all-to-all-start.3) | async-done | bytes 1048608 | tf_op jit(solution)/shard_map/all_to_all | solution.py:12
  180.4 2.2 convolution_convert_fusion.3
  183.4 9.8 %all_to_all.41 = bf16[4,64,768]{2,1,0:T(8,128)(2,1)S(1)} all-to-all(bf16[4,64,768]{2,1,0:T(8,128)(2,1)S(1)} %bitcast.94), channel_id=1, replica_groups=mesh['zl'=8,'y'=4,'c'=2,'zh'=2,'x'=4] {'y'}, dimensions={0} | all-to-all | bytes 786432 | tf_op jit(solution)/shard_map/all_to_all | solution.py:104
  193.3 16.5 %all_to_all.42 = bf16[8,8,768]{2,1,0:T(8,128)(2,1)} all-to-all(bf16[8,8,768]{2,1,0:T(8,128)(2,1)S(1)} %fusion.5), channel_id=1, replica_groups=mesh['zl'=8,'y'=4,'c'=2,'zh'=2,'x'=4] {'zl'}, dimensions={0} | all-to-all | bytes 196608 | tf_op jit(solution)/shard_map/all_to_all | solution.py:107
  209.8 4.6 %all-to-all-start.7 = ((bf16[8,8,768]{2,1,0:T(8,128)(2,1)}), bf16[8,8,768]{2,1,0:T(8,128)(2,1)S(1)}, u32[]{:S(2)}, u32[]{:S(2)}) async-start(bf16[8,8,768]{2,1,0:T(8,128)(2,1)} %all_to_all.42), calls=%async_computation.7 | async-start | bytes 196608 | tf_op jit(solution)/shard_map/all_to_all | solution.py:110
  214.5 16.4 %all-to-all-done.7 = bf16[8,8,768]{2,1,0:T(8,128)(2,1)S(1)} async-done(((bf16[8,8,768]{2,1,0:T(8,128)(2,1)}), bf16[8,8,768]{2,1,0:T(8,128)(2,1)S(1)}, u32[]{:S(2)}, u32[]{:S(2)}) %all-to-all-start.7) | async-done | bytes 98336 | tf_op jit(solution)/shard_map/all_to_all | solution.py:110
  (50 shorter events, 9.1 us)
Async XLA Ops:
  3.6 39.3 %all-to-all-start = ((bf16[16,16,896]{2,1,0:T(8,128)(2,1)}), bf16[16,16,896]{2,1,0:T(8,128)(2,1)S(1)}, u32[]{:S(2)}, u32[]{:S(2)}) async-start(bf16[16,16,896]{2,1,0:T(8,128)(2,1)} %broadcast_in_dim.6), calls=%async_computation | async-start | bytes 917504 | tf_op jit(solution)/shard_map/all_to_all | solution.py:12
  60.5 38.7 %all-to-all-start.2 = ((bf16[4,64,6144]{2,1,0:T(8,128)(2,1)}), bf16[4,64,6144]{2,1,0:T(8,128)(2,1)S(1)}, u32[]{:S(2)}, u32[]{:S(2)}) async-start(bf16[4,64,6144]{2,1,0:T(8,128)(2,1)} %broadcast_in_dim.7), calls=%async_computation.2 | async-start | bytes 6291456 | tf_op jit(solution)/shard_map/all_to_all | solution.py:12
  64.9 41.2 %collective-permute-start = (bf16[6144,128]{1,0:T(8,128)(2,1)}, bf16[6144,128]{1,0:T(8,128)(2,1)}, u32[]{:S(2)}, u32[]{:S(2)}) collective-permute-start(bf16[6144,128]{1,0:T(8,128)(2,1)} %bitcast.95), channel_id=1, source_target_pairs={{0,8},{8,0},{1,9},{9,1},{2,10},{10,2},{3,11},{11,3},{4,12},{12,4},... | collective-permute-start | bytes 4718600 | tf_op jit(solution)/shard_map/ppermute | solution.py:37
  66.8 43.2 %collective-permute-start.1 = (bf16[6144,128]{1,0:T(8,128)(2,1)}, bf16[6144,128]{1,0:T(8,128)(2,1)}, u32[]{:S(2)}, u32[]{:S(2)}) collective-permute-start(bf16[6144,128]{1,0:T(8,128)(2,1)} %bitcast.96), channel_id=1, source_target_pairs={{0,8},{8,0},{1,9},{9,1},{2,10},{10,2},{3,11},{11,3},{4,12},{12,4},... | collective-permute-start | bytes 4718600 | tf_op jit(solution)/shard_map/ppermute | solution.py:38
  99.2 21.0 %all-to-all-start.4 = ((bf16[4,96,2048]{2,1,0:T(8,128)(2,1)}), bf16[4,96,2048]{2,1,0:T(8,128)(2,1)}, u32[]{:S(2)}, u32[]{:S(2)}) async-start(bf16[4,96,2048]{2,1,0:T(8,128)(2,1)} %reshape.126), calls=%async_computation.4 | async-start | bytes 3145728 | tf_op jit(solution)/shard_map/all_to_all | solution.py:41
  106.1 2.7 %copy-start = (bf16[1,6144,128]{2,1,0:T(8,128)(2,1)S(1)}, bf16[1,6144,128]{2,1,0:T(8,128)(2,1)}, u32[]{:S(2)}) copy-start(bf16[1,6144,128]{2,1,0:T(8,128)(2,1)} %param.10) | copy-start | bytes 4718596
  121.2 59.2 %all-to-all-start.3 = ((bf16[8,256,256]{1,2,0:T(8,128)(2,1)}), bf16[8,256,256]{1,2,0:T(8,128)(2,1)S(1)}, u32[]{:S(2)}, u32[]{:S(2)}) async-start(bf16[8,256,256]{1,2,0:T(8,128)(2,1)} %broadcast_in_dim.8), calls=%async_computation.3 | async-start | bytes 2097152 | tf_op jit(solution)/shard_map/all_to_all | solution.py:12
  135.3 47.3 %collective-permute-start.2 = (bf16[384,2048]{1,0:T(8,128)(2,1)}, bf16[384,2048]{1,0:T(8,128)(2,1)S(1)}, u32[]{:S(2)}, u32[]{:S(2)}) collective-permute-start(bf16[384,2048]{1,0:T(8,128)(2,1)} %bitcast.22), channel_id=1, source_target_pairs={{0,8},{8,0},{1,9},{9,1},{2,10},{10,2},{3,11},{11,3},{4,12},{12,4},... | collective-permute-start | bytes 4718600 | tf_op jit(solution)/shard_map/ppermute | solution.py:44
  183.4 31.0 %copy-start.1 = (f32[16,2]{0,1:T(2,128)S(1)}, f32[16,2]{0,1:T(2,128)}, u32[]{:S(2)}) copy-start(f32[16,2]{0,1:T(2,128)} %param.8) | copy-start | bytes 388
  209.8 21.1 %all-to-all-start.7 = ((bf16[8,8,768]{2,1,0:T(8,128)(2,1)}), bf16[8,8,768]{2,1,0:T(8,128)(2,1)S(1)}, u32[]{:S(2)}, u32[]{:S(2)}) async-start(bf16[8,8,768]{2,1,0:T(8,128)(2,1)} %all_to_all.42), calls=%async_computation.7 | async-start | bytes 196608 | tf_op jit(solution)/shard_map/all_to_all | solution.py:110

commit v2 on v1

--- a/solution.py
+++ b/solution.py
@@ -6,6 +6,14 @@
 AXES = ("zl", "y", "c", "zh", "x")
 SIZES = (8, 4, 2, 2, 4)
 SWAP = [(0, 1), (1, 0)]
+
+
+def step(count, shift):
+    return [(i, (i + shift) % count) for i in range(count)]
+
+
+def flip(axis_size, mask):
+    return [(i, i ^ mask) for i in range(axis_size)]
 
 
 def everyone(value, axis, count):
@@ -37,12 +45,30 @@
     gate_far = lax.ppermute(gate_own, "c", SWAP)
     up_far = lax.ppermute(up_own, "c", SWAP)
     features = w_down_t.shape[1]
-    down = w_down_t[0].reshape(features, zl, y, c * units).transpose(2, 0, 1, 3)
-    down = lax.all_to_all(
-        down.reshape(y, features, zl * c * units), "y", 0, 0, tiled=True
-    ).reshape(y * features, zl * c * units)
-    down_far = lax.ppermute(down, "c", SWAP)
+    z_here = lax.axis_index("zl")
+    order = [q ^ k for k in range(4) for q in (0, 4)]
+    span = c * units
+    y_here = lax.axis_index("y")
 
+    def columns(shift):
+        at = ((y_here + shift) % y) * span
+        return jnp.concatenate(
+            [
+                lax.dynamic_slice_in_dim(
+                    w_down_t[0], (z_here ^ j) * (y * span) + at, span, 1
+                )
+                for j in order
+            ],
+            axis=1,
+        )
+
+    down = jnp.zeros((y, features, zl * span), bf16)
+    for k in range(y):
+        moved = columns(k)
+        if k:
+            moved = lax.ppermute(moved, "y", step(y, k))
+        down = lax.dynamic_update_slice_in_dim(down, moved[None], (y_here - k) % y, 0)
+    down = down.reshape(y * features, zl * span)
     slot = slot_numbers(expert_ids, capacity)
     tail = jnp.pad(slot, ((0, 0), (0, 126)), constant_values=0).astype(bf16)
     seen = everyone(jnp.concatenate([tokens, tail], axis=1), ("zh", "zl"), zh * zl)
@@ -72,35 +98,56 @@
         axis=1,
     )
     arrived = lax.all_to_all(slots, "x", 0, 0, tiled=True)
+    arrived, down, gate_far, up_far = lax.optimization_barrier(
+        (arrived, down, gate_far, up_far)
+    )
     piece = jnp.concatenate(
         [arrived[i, h * rows : (h + 1) * rows] for h in range(zh) for i in range(x)],
         axis=1,
     )
-    piece = everyone(piece, "y", y).reshape(y * rows, model)
+    down_far = lax.ppermute(down, "c", SWAP)
+    up1 = lax.ppermute(piece, "y", step(y, 1))
+    dn1 = lax.ppermute(piece, "y", step(y, -1))
+    half = rows // 2
+    far_a = lax.ppermute(up1[:half], "y", step(y, 1))
+    far_b = lax.ppermute(dn1[half:], "y", step(y, -1))
+    blocks = (piece, up1, dn1, jnp.concatenate([far_a, far_b], axis=0))
+    first = lax.axis_index("c") == 0
 
-    def act(w1, w2):
-        gate = jnp.dot(piece, w1, preferred_element_type=f32)
-        up = jnp.dot(piece, w2, preferred_element_type=f32)
+    def act(rows_in, w1, w2):
+        gate = jnp.dot(rows_in, w1, preferred_element_type=f32)
+        up = jnp.dot(rows_in, w2, preferred_element_type=f32)
         return (jax.nn.silu(gate) * up).astype(bf16)
 
-    first = lax.axis_index("c") == 0
-    own, far = act(gate_own, up_own), act(gate_far, up_far)
+    def out(hidden, w):
+        total = 0.0
+        for k, h in enumerate(hidden):
+            total = total + lax.dot_general(
+                h,
+                w[:, k * 2 * span : (k + 1) * 2 * span],
+                (((1,), (1,)), ((), ())),
+                preferred_element_type=f32,
+            )
+        return total.astype(bf16)
+
+    taken = jnp.concatenate(blocks, axis=0)
+    own, far = act(taken, gate_own, up_own), act(taken, gate_far, up_far)
     hidden = jnp.concatenate(
         [jnp.where(first, own, far), jnp.where(first, far, own)], axis=1
     )
-    hidden = everyone(hidden, "zl", zl)
-    hidden = hidden.transpose(1, 0, 2).reshape(y * rows, zl * c * units)
-
-    def out(w):
-        part = lax.dot_general(
-            hidden, w, (((1,), (1,)), ((), ())), preferred_element_type=f32
-        )
-        return part.astype(bf16)
-
-    own, far = out(down), out(down_far)
+    other = lax.ppermute(hidden, "zl", flip(zl, 4))
+    pair = jnp.concatenate([hidden, other], axis=1)
+    pairs = [pair] + [lax.ppermute(pair, "zl", flip(zl, k)) for k in (1, 2, 3)]
+    own, far = out(pairs, down), out(pairs, down_far)
     part = jnp.concatenate(
         [jnp.where(first, own, far), jnp.where(first, far, own)], axis=1
-    ).reshape(y, rows, width)
+    )
+    parts = [part[n * rows : (n + 1) * rows] for n in range(y)]
+
+    part = jnp.stack([parts[0], parts[2], parts[3], parts[1]])
+    part = lax.dynamic_slice_in_dim(
+        jnp.concatenate([part, part]), (y - y_here) % y, y, 0
+    )
     part = lax.all_to_all(part, "y", 0, 0, tiled=True).astype(f32)
     result = ((part[0] + part[1]) + (part[2] + part[3])).astype(bf16)
 
@@ -108,6 +155,7 @@
         result.reshape(zl, capacity, width), "zl", 0, 0, tiled=True
     )
     result = lax.all_to_all(result, ("zh", "x"), 0, 0, tiled=True)
+    result, slot, gate_probs = lax.optimization_barrier((result, slot, gate_probs))
     result = result.reshape(experts * capacity, width)
 
     every = jnp.arange(experts * capacity, dtype=jnp.int32)

time: 233 us -> 211 us (0.906)
  waiting for transfers between devices: 111 us -> 52.1 us
  starting transfers between devices: 49 us -> 68.7 us
  blocking collectives: 40.8 us -> 56.4 us
  local copies, waits for them, and re-layouts: 16.6 us -> 10.4 us
  matrix products: 13 us -> 18.2 us
    all_to_all x3 -> x1, waiting for transfers between devices: 86.6 us -> 1.07 us  [everyone(): lax.all_to_all(jnp.broadcast_to(value[None], (count,) + value.shape), axi...]
    ppermute x0 -> x11, starting transfers between devices: none -> 43 us  [the longest x3 11.5 us: per_device(): moved = lax.ppermute(moved, 'y', step(y, k))]
    ppermute x0 -> x11, waiting for transfers between devices: none -> 39.7 us  [the longest x3 16.1 us: per_device(): pairs = [pair] + [lax.ppermute(pair, 'zl', flip(zl, k)) for k in (1, 2, 3)]]
    all_to_all x3 -> x1, starting transfers between devices: 33.8 us -> 15.2 us  [everyone(): lax.all_to_all(jnp.broadcast_to(value[None], (count,) + value.shape), axi...]
    all_to_all x2 -> x1, waiting for transfers between devices: 23.9 us -> 11.3 us  [per_device(): arrived = lax.all_to_all(slots, 'x', 0, 0, tiled=True)]
    all_to_all x1, blocking collectives: 14.5 us -> 25 us  [per_device(): result = lax.all_to_all(result, ('zh', 'x'), 0, 0, tiled=True)]
    another operation x2 -> x0, local copies, waits for them, and re-layouts: 6.7 us -> none  [per_device(): down = w_down_t[0].reshape(features, zl, y, c * units).transpose(2, 0, 1, 3)]
    dot_general x6 -> x12, matrix products: 12 us -> 17.2 us  [the longest x8 6.78 us: out(): lax.dot_general(h, w[:, k * 2 * span:(k + 1) * 2 * span], (((1,), (1,)),...]
  transfers between devices with their start and end apart: 8 -> 16, of which waited for: 5 -> 9; matrix products, arithmetic and copies ran while one was open for 9% -> 11% of each run, Pallas kernels for 0% -> 0%
where the time goes in v2:
time: 211 us; the launch traced here: 210 us
  starting transfers between devices  68.7 us (33%)
  blocking collectives  56.4 us (27%)
  waiting for transfers between devices  52.1 us (25%)
  matrix products  18.2 us (9%)
  local copies, waits for them, and re-layouts  10.4 us (5%)
  other arithmetic  2.9 us (1%)
    all_to_all x1, blocking collectives, per_device(): result = lax.all_to_all(result, ('zh', 'x'), 0, 0, tiled=True)  25 us
    all_to_all x1, blocking collectives, per_device(): lax.all_to_all(result.reshape(zl, capacity, width), 'zl', 0, 0, tiled=True)  19.3 us
    ppermute x3, waiting for transfers between devices, per_device(): pairs = [pair] + [lax.ppermute(pair, 'zl', flip(zl, k)) for k in (1, 2, 3)]  16.1 us
    all_to_all x1, starting transfers between devices, everyone(): lax.all_to_all(jnp.broadcast_to(value[None], (count,) + value.shape), axi...  15.2 us
    all_to_all x1, blocking collectives, per_device(): part = lax.all_to_all(part, 'y', 0, 0, tiled=True).astype(f32)  12.1 us
    ppermute x3, starting transfers between devices, per_device(): moved = lax.ppermute(moved, 'y', step(y, k))  11.5 us
    all_to_all x1, waiting for transfers between devices, per_device(): arrived = lax.all_to_all(slots, 'x', 0, 0, tiled=True)  11.3 us
    ppermute x1, waiting for transfers between devices, per_device(): up1 = lax.ppermute(piece, 'y', step(y, 1))  11 us
  transfers between devices with their start and end apart: 16, of which 9 were waited for; matrix products, arithmetic and copies ran while one was open for 11% of the time, Pallas kernels for 0%

profile of v2, /device:TPU:32, one launch (start us, length us, event | category | flops | bytes accessed | tf_op | source)
XLA Modules:
  0.0 209.5 jit_solution(13410455862342457448)
XLA Ops:
  3.7 15.2 %all-to-all-start = ((bf16[16,16,896]{2,1,0:T(8,128)(2,1)}), bf16[16,16,896]{2,1,0:T(8,128)(2,1)S(1)}, u32[]{:S(2)}, u32[]{:S(2)}) async-start(bf16[16,16,896]{2,1,0:T(8,128)(2,1)} %broadcast_in_dim.12), calls=%async_computation | async-start | bytes 917504 | tf_op jit(solution)/shard_map/all_to_all | solution.py:20
  24.5 3.5 %collective-permute-start = (bf16[96,2048]{1,0:T(8,128)(2,1)}, bf16[96,2048]{1,0:T(8,128)(2,1)}, u32[]{:S(2)}, u32[]{:S(2)}) collective-permute-start(bf16[96,2048]{1,0:T(8,128)(2,1)} %get-tuple-element.29), channel_id=1, source_target_pairs={{0,16},{16,32},{32,48},{48,0},{1,17},{17,33},{33,49},{49,1},{2,18}... | collective-permute-start | bytes 1179656 | tf_op jit(solution)/shard_map/ppermute | solution.py:69
  27.9 4.8 %collective-permute-start.1 = (bf16[96,2048]{1,0:T(8,128)(2,1)}, bf16[96,2048]{1,0:T(8,128)(2,1)S(1)}, u32[]{:S(2)}, u32[]{:S(2)}) collective-permute-start(bf16[96,2048]{1,0:T(8,128)(2,1)} %get-tuple-element.28), channel_id=1, source_target_pairs={{0,32},{16,48},{32,0},{48,16},{1,33},{17,49},{33,1},{49,17},{2,34}... | collective-permute-start | bytes 1179656 | tf_op jit(solution)/shard_map/ppermute | solution.py:69
  32.8 3.3 %collective-permute-start.2 = (bf16[96,2048]{1,0:T(8,128)(2,1)}, bf16[96,2048]{1,0:T(8,128)(2,1)S(1)}, u32[]{:S(2)}, u32[]{:S(2)}) collective-permute-start(bf16[96,2048]{1,0:T(8,128)(2,1)} %get-tuple-element.27), channel_id=1, source_target_pairs={{0,48},{16,0},{32,16},{48,32},{1,49},{17,1},{33,17},{49,33},{2,50}... | collective-permute-start | bytes 1179656 | tf_op jit(solution)/shard_map/ppermute | solution.py:69
  37.9 2.4 %collective-permute-start.4 = (bf16[6144,128]{1,0:T(8,128)(2,1)}, bf16[6144,128]{1,0:T(8,128)(2,1)}, u32[]{:S(2)}, u32[]{:S(2)}) collective-permute-start(bf16[6144,128]{1,0:T(8,128)(2,1)} %bitcast.44), channel_id=1, source_target_pairs={{0,8},{8,0},{1,9},{9,1},{2,10},{10,2},{3,11},{11,3},{4,12},{12,4},... | collective-permute-start | bytes 4718600 | tf_op jit(solution)/shard_map/ppermute | solution.py:46
  44.8 4.3 %all-to-all-start.1 = ((bf16[4,128,768]{2,1,0:T(8,128)(2,1)}), bf16[4,128,768]{2,1,0:T(8,128)(2,1)S(1)}, u32[]{:S(2)}, u32[]{:S(2)}) async-start(bf16[4,128,768]{2,1,0:T(8,128)(2,1)} %pad_maximum_fusion), calls=%async_computation.1 | async-start | bytes 1572864 | tf_op jit(solution)/shard_map/all_to_all | solution.py:100
  49.2 11.3 %all-to-all-done.1 = bf16[4,128,768]{2,1,0:T(8,128)(2,1)S(1)} async-done(((bf16[4,128,768]{2,1,0:T(8,128)(2,1)}), bf16[4,128,768]{2,1,0:T(8,128)(2,1)S(1)}, u32[]{:S(2)}, u32[]{:S(2)}) %all-to-all-start.1) | async-done | bytes 786464 | tf_op jit(solution)/shard_map/all_to_all | solution.py:100
  60.7 2.6 %collective-permute-start.5 = (bf16[64,6144]{1,0:T(8,128)(2,1)S(1)}, bf16[64,6144]{1,0:T(8,128)(2,1)S(1)}, u32[]{:S(2)}, u32[]{:S(2)}) collective-permute-start(bf16[64,6144]{1,0:T(8,128)(2,1)S(1)} %get-tuple-element.59), channel_id=1, source_target_pairs={{0,16},{16,32},{32,48},{48,0},{1,17},{17,33},{33,49},{49,1},{2,18}... | collective-permute-start | bytes 2359304 | tf_op jit(solution)/shard_map/ppermute | solution.py:109
  63.3 4.5 %collective-permute-start.6 = (bf16[64,6144]{1,0:T(8,128)(2,1)S(1)}, bf16[64,6144]{1,0:T(8,128)(2,1)S(1)}, u32[]{:S(2)}, u32[]{:S(2)}) collective-permute-start(bf16[64,6144]{1,0:T(8,128)(2,1)S(1)} %get-tuple-element.59), channel_id=1, source_target_pairs={{0,48},{16,0},{32,16},{48,32},{1,49},{17,1},{33,17},{49,33},{2,50}... | collective-permute-start | bytes 2359304 | tf_op jit(solution)/shard_map/ppermute | solution.py:110
  69.8 11.0 %collective-permute-done.5 = bf16[64,6144]{1,0:T(8,128)(2,1)S(1)} collective-permute-done((bf16[64,6144]{1,0:T(8,128)(2,1)S(1)}, bf16[64,6144]{1,0:T(8,128)(2,1)S(1)}, u32[]{:S(2)}, u32[]{:S(2)}) %collective-permute-start.5) | collective-permute-done | bytes 786464 | tf_op jit(solution)/shard_map/ppermute | solution.py:109
  82.7 5.1 %collective-permute-start.8 = (bf16[32,6144]{1,0:T(8,128)(2,1)S(1)}, bf16[32,6144]{1,0:T(8,128)(2,1)S(1)}, u32[]{:S(2)}, u32[]{:S(2)}) collective-permute-start(bf16[32,6144]{1,0:T(8,128)(2,1)S(1)} %slice.146), channel_id=1, source_target_pairs={{0,48},{16,0},{32,16},{48,32},{1,49},{17,1},{33,17},{49,33},{2,50}... | collective-permute-start | bytes 1179656 | tf_op jit(solution)/shard_map/ppermute | solution.py:113
  88.0 3.6 %collective-permute-done.7 = bf16[32,6144]{1,0:T(8,128)(2,1)S(1)} collective-permute-done((bf16[32,6144]{1,0:T(8,128)(2,1)S(1)}, bf16[32,6144]{1,0:T(8,128)(2,1)S(1)}, u32[]{:S(2)}, u32[]{:S(2)}) %collective-permute-start.7) | collective-permute-done | bytes 393248 | tf_op jit(solution)/shard_map/ppermute | solution.py:112
  93.2 2.6 %fusion.44 = f32[256,128]{0,1:T(8,128)S(1)} fusion(bf16[256,6144]{1,0:T(8,128)(2,1)S(1)} %constant_dynamic-update-slice_fusion.40, bf16[1,6144,128]{2,1,0:T(8,128)(2,1)} %param.9), kind=kOutput, calls=%fused_computation.160 | convolution fusion | flops 402653184 | bytes 4849664 | tf_op jit(solution)/shard_map/dot_general | solution.py:118
  95.8 2.6 %fusion.48 = f32[256,128]{0,1:T(8,128)S(1)} fusion(bf16[256,6144]{1,0:T(8,128)(2,1)S(1)} %constant_dynamic-update-slice_fusion.40, bf16[6144,128]{1,0:T(8,128)(2,1)} %collective-permute-done.3), kind=kOutput, calls=%fused_computation.163 | convolution fusion | flops 402653184 | bytes 4849664 | tf_op jit(solution)/shard_map/dot_general | solution.py:118
  98.4 2.6 %multiply_convert_fusion.1 = bf16[256,128]{0,1:T(8,128)(2,1)S(1)} fusion(f32[256,128]{0,1:T(8,128)S(1)} %fusion.44, bf16[256,6144]{1,0:T(8,128)(2,1)S(1)} %constant_dynamic-update-slice_fusion.40, bf16[1,6144,128]{2,1,0:T(8,128)(2,1)} %param.10), kind=kOutput, calls=%fused_computation.50 | convolution fusion | flops 402849792 | bytes 4915200 | tf_op jit(solution)/shard_map/dot_general | solution.py:119
  101.0 2.6 %broadcast_select_fusion.3 = (bf16[256,128]{0,1:T(8,128)(2,1)S(1)}, bf16[256,128]{0,1:T(8,128)(2,1)S(1)}) fusion(bf16[256,128]{0,1:T(8,128)(2,1)S(1)} %multiply_convert_fusion.1, pred[]{:T(512)S(6)} %eq.103, f32[256,128]{0,1:T(8,128)S(1)} %fusion.48, bf16[256,6144]{1,0:T(8,128)(2,1)S(1)} %constant_dynamic-update-slice_fusion.40, ...), kind=kOutput, calls=%fused_computation.127 | convolution fusion | flops 402882560 | bytes 5046273 | tf_op jit(solution)/shard_map/dot_general | solution.py:119
  103.7 7.3 %collective-permute-start.9 = (bf16[256,256]{0,1:T(8,128)(2,1)S(1)}, bf16[256,256]{0,1:T(8,128)(2,1)S(1)}, u32[]{:S(2)}, u32[]{:S(2)}) collective-permute-start(bf16[256,256]{0,1:T(8,128)(2,1)S(1)} %pad_maximum_fusion.2), channel_id=1, source_target_pairs={{0,256},{64,320},{128,384},{192,448},{256,0},{320,64},{384,128},{4... | collective-permute-start | bytes 393224 | tf_op jit(solution)/shard_map/ppermute | solution.py:138
  111.0 7.5 %collective-permute-done.9 = bf16[256,256]{0,1:T(8,128)(2,1)S(1)} collective-permute-done((bf16[256,256]{0,1:T(8,128)(2,1)S(1)}, bf16[256,256]{0,1:T(8,128)(2,1)S(1)}, u32[]{:S(2)}, u32[]{:S(2)}) %collective-permute-start.9) | collective-permute-done | bytes 131104 | tf_op jit(solution)/shard_map/ppermute | solution.py:138
  118.6 4.7 %collective-permute-start.10 = (bf16[256,512]{0,1:T(8,128)(2,1)S(1)}, bf16[256,512]{0,1:T(8,128)(2,1)S(1)}, u32[]{:S(2)}, u32[]{:S(2)}) collective-permute-start(bf16[256,512]{0,1:T(8,128)(2,1)S(1)} %pad_maximum_fusion.1), channel_id=1, source_target_pairs={{0,64},{64,0},{128,192},{192,128},{256,320},{320,256},{384,448},{4... | collective-permute-start | bytes 786440 | tf_op jit(solution)/shard_map/ppermute | solution.py:140
  125.2 3.4 %collective-permute-start.12 = (bf16[256,512]{0,1:T(8,128)(2,1)S(1)}, bf16[256,512]{0,1:T(8,128)(2,1)S(1)}, u32[]{:S(2)}, u32[]{:S(2)}) collective-permute-start(bf16[256,512]{0,1:T(8,128)(2,1)S(1)} %pad_maximum_fusion.1), channel_id=1, source_target_pairs={{0,192},{64,128},{128,64},{192,0},{256,448},{320,384},{384,320},{4... | collective-permute-start | bytes 786440 | tf_op jit(solution)/shard_map/ppermute | solution.py:140
  130.8 12.0 %collective-permute-done.11 = bf16[256,512]{0,1:T(8,128)(2,1)S(1)} collective-permute-done((bf16[256,512]{0,1:T(8,128)(2,1)S(1)}, bf16[256,512]{0,1:T(8,128)(2,1)S(1)}, u32[]{:S(2)}, u32[]{:S(2)}) %collective-permute-start.11) | collective-permute-done | bytes 262176 | tf_op jit(solution)/shard_map/ppermute | solution.py:140
  151.7 12.1 %all_to_all.25 = bf16[4,64,768]{2,1,0:T(8,128)(2,1)S(1)} all-to-all(bf16[4,64,768]{2,1,0:T(8,128)(2,1)S(1)} %constant_dynamic-slice_fusion), channel_id=1, replica_groups=mesh['zl'=8,'y'=4,'c'=2,'zh'=2,'x'=4] {'y'}, dimensions={0} | all-to-all | bytes 786432 | tf_op jit(solution)/shard_map/all_to_all | solution.py:151
  164.0 19.3 %all_to_all.26 = bf16[8,8,768]{2,1,0:T(8,128)(2,1)S(1)} all-to-all(bf16[8,8,768]{2,1,0:T(8,128)(2,1)S(1)} %fusion.24), channel_id=1, replica_groups=mesh['zl'=8,'y'=4,'c'=2,'zh'=2,'x'=4] {'zl'}, dimensions={0} | all-to-all | bytes 196608 | tf_op jit(solution)/shard_map/all_to_all | solution.py:154
  183.2 25.0 %all_to_all.27 = bf16[8,8,768]{2,1,0:T(8,128)(2,1)S(1)} all-to-all(bf16[8,8,768]{2,1,0:T(8,128)(2,1)S(1)} %all_to_all.26), channel_id=1, replica_groups=mesh['zl'=8,'y'=4,'c'=2,'zh'=2,'x'=4] {'zh','x'}, dimensions={0} | all-to-all | bytes 196608 | tf_op jit(solution)/shard_map/all_to_all | solution.py:157
  (102 shorter events, 35.5 us)
Async XLA Ops:
  0.0 18.9 %copy-start = (bf16[1,96,8192]{2,1,0:T(8,128)(2,1)S(1)}, bf16[1,96,8192]{2,1,0:T(8,128)(2,1)}, u32[]{:S(2)}) copy-start(bf16[1,96,8192]{2,1,0:T(8,128)(2,1)} %param.11) | copy-start | bytes 4718596
  3.7 39.3 %all-to-all-start = ((bf16[16,16,896]{2,1,0:T(8,128)(2,1)}), bf16[16,16,896]{2,1,0:T(8,128)(2,1)S(1)}, u32[]{:S(2)}, u32[]{:S(2)}) async-start(bf16[16,16,896]{2,1,0:T(8,128)(2,1)} %broadcast_in_dim.12), calls=%async_computation | async-start | bytes 917504 | tf_op jit(solution)/shard_map/all_to_all | solution.py:20
  24.5 16.4 %collective-permute-start = (bf16[96,2048]{1,0:T(8,128)(2,1)}, bf16[96,2048]{1,0:T(8,128)(2,1)}, u32[]{:S(2)}, u32[]{:S(2)}) collective-permute-start(bf16[96,2048]{1,0:T(8,128)(2,1)} %get-tuple-element.29), channel_id=1, source_target_pairs={{0,16},{16,32},{32,48},{48,0},{1,17},{17,33},{33,49},{49,1},{2,18}... | collective-permute-start | bytes 1179656 | tf_op jit(solution)/shard_map/ppermute | solution.py:69
  27.9 21.2 %collective-permute-start.1 = (bf16[96,2048]{1,0:T(8,128)(2,1)}, bf16[96,2048]{1,0:T(8,128)(2,1)S(1)}, u32[]{:S(2)}, u32[]{:S(2)}) collective-permute-start(bf16[96,2048]{1,0:T(8,128)(2,1)} %get-tuple-element.28), channel_id=1, source_target_pairs={{0,32},{16,48},{32,0},{48,16},{1,33},{17,49},{33,1},{49,17},{2,34}... | collective-permute-start | bytes 1179656 | tf_op jit(solution)/shard_map/ppermute | solution.py:69
  32.8 16.4 %collective-permute-start.2 = (bf16[96,2048]{1,0:T(8,128)(2,1)}, bf16[96,2048]{1,0:T(8,128)(2,1)S(1)}, u32[]{:S(2)}, u32[]{:S(2)}) collective-permute-start(bf16[96,2048]{1,0:T(8,128)(2,1)} %get-tuple-element.27), channel_id=1, source_target_pairs={{0,48},{16,0},{32,16},{48,32},{1,49},{17,1},{33,17},{49,33},{2,50}... | collective-permute-start | bytes 1179656 | tf_op jit(solution)/shard_map/ppermute | solution.py:69
  36.0 13.2 %collective-permute-start.3 = (bf16[6144,128]{1,0:T(8,128)(2,1)}, bf16[6144,128]{1,0:T(8,128)(2,1)}, u32[]{:S(2)}, u32[]{:S(2)}) collective-permute-start(bf16[6144,128]{1,0:T(8,128)(2,1)} %bitcast.43), channel_id=1, source_target_pairs={{0,8},{8,0},{1,9},{9,1},{2,10},{10,2},{3,11},{11,3},{4,12},{12,4},... | collective-permute-start | bytes 4718600 | tf_op jit(solution)/shard_map/ppermute | solution.py:45
  37.9 11.3 %collective-permute-start.4 = (bf16[6144,128]{1,0:T(8,128)(2,1)}, bf16[6144,128]{1,0:T(8,128)(2,1)}, u32[]{:S(2)}, u32[]{:S(2)}) collective-permute-start(bf16[6144,128]{1,0:T(8,128)(2,1)} %bitcast.44), channel_id=1, source_target_pairs={{0,8},{8,0},{1,9},{9,1},{2,10},{10,2},{3,11},{11,3},{4,12},{12,4},... | collective-permute-start | bytes 4718600 | tf_op jit(solution)/shard_map/ppermute | solution.py:46
  44.8 15.7 %all-to-all-start.1 = ((bf16[4,128,768]{2,1,0:T(8,128)(2,1)}), bf16[4,128,768]{2,1,0:T(8,128)(2,1)S(1)}, u32[]{:S(2)}, u32[]{:S(2)}) async-start(bf16[4,128,768]{2,1,0:T(8,128)(2,1)} %pad_maximum_fusion), calls=%async_computation.1 | async-start | bytes 1572864 | tf_op jit(solution)/shard_map/all_to_all | solution.py:100
  60.7 20.1 %collective-permute-start.5 = (bf16[64,6144]{1,0:T(8,128)(2,1)S(1)}, bf16[64,6144]{1,0:T(8,128)(2,1)S(1)}, u32[]{:S(2)}, u32[]{:S(2)}) collective-permute-start(bf16[64,6144]{1,0:T(8,128)(2,1)S(1)} %get-tuple-element.59), channel_id=1, source_target_pairs={{0,16},{16,32},{32,48},{48,0},{1,17},{17,33},{33,49},{49,1},{2,18}... | collective-permute-start | bytes 2359304 | tf_op jit(solution)/shard_map/ppermute | solution.py:109
  63.3 19.5 %collective-permute-start.6 = (bf16[64,6144]{1,0:T(8,128)(2,1)S(1)}, bf16[64,6144]{1,0:T(8,128)(2,1)S(1)}, u32[]{:S(2)}, u32[]{:S(2)}) collective-permute-start(bf16[64,6144]{1,0:T(8,128)(2,1)S(1)} %get-tuple-element.59), channel_id=1, source_target_pairs={{0,48},{16,0},{32,16},{48,32},{1,49},{17,1},{33,17},{49,33},{2,50}... | collective-permute-start | bytes 2359304 | tf_op jit(solution)/shard_map/ppermute | solution.py:110
  67.8 75.4 %collective-permute-start.13 = (bf16[384,2048]{1,0:T(8,128)(2,1)S(1)}, bf16[384,2048]{1,0:T(8,128)(2,1)}, u32[]{:S(2)}, u32[]{:S(2)}) collective-permute-start(bf16[384,2048]{1,0:T(8,128)(2,1)S(1)} %bitcast.165), channel_id=1, source_target_pairs={{0,8},{8,0},{1,9},{9,1},{2,10},{10,2},{3,11},{11,3},{4,12},{12,4},... | collective-permute-start | bytes 4718600 | tf_op jit(solution)/shard_map/ppermute | solution.py:108
  80.8 10.9 %collective-permute-start.7 = (bf16[32,6144]{1,0:T(8,128)(2,1)S(1)}, bf16[32,6144]{1,0:T(8,128)(2,1)S(1)}, u32[]{:S(2)}, u32[]{:S(2)}) collective-permute-start(bf16[32,6144]{1,0:T(8,128)(2,1)S(1)} %slice.145), channel_id=1, source_target_pairs={{0,16},{16,32},{32,48},{48,0},{1,17},{17,33},{33,49},{49,1},{2,18}... | collective-permute-start | bytes 1179656 | tf_op jit(solution)/shard_map/ppermute | solution.py:112
  82.7 10.4 %collective-permute-start.8 = (bf16[32,6144]{1,0:T(8,128)(2,1)S(1)}, bf16[32,6144]{1,0:T(8,128)(2,1)S(1)}, u32[]{:S(2)}, u32[]{:S(2)}) collective-permute-start(bf16[32,6144]{1,0:T(8,128)(2,1)S(1)} %slice.146), channel_id=1, source_target_pairs={{0,48},{16,0},{32,16},{48,32},{1,49},{17,1},{33,17},{49,33},{2,50}... | collective-permute-start | bytes 1179656 | tf_op jit(solution)/shard_map/ppermute | solution.py:113
  103.7 14.9 %collective-permute-start.9 = (bf16[256,256]{0,1:T(8,128)(2,1)S(1)}, bf16[256,256]{0,1:T(8,128)(2,1)S(1)}, u32[]{:S(2)}, u32[]{:S(2)}) collective-permute-start(bf16[256,256]{0,1:T(8,128)(2,1)S(1)} %pad_maximum_fusion.2), channel_id=1, source_target_pairs={{0,256},{64,320},{128,384},{192,448},{256,0},{320,64},{384,128},{4... | collective-permute-start | bytes 393224 | tf_op jit(solution)/shard_map/ppermute | solution.py:138
  118.6 11.9 %collective-permute-start.10 = (bf16[256,512]{0,1:T(8,128)(2,1)S(1)}, bf16[256,512]{0,1:T(8,128)(2,1)S(1)}, u32[]{:S(2)}, u32[]{:S(2)}) collective-permute-start(bf16[256,512]{0,1:T(8,128)(2,1)S(1)} %pad_maximum_fusion.1), channel_id=1, source_target_pairs={{0,64},{64,0},{128,192},{192,128},{256,320},{320,256},{384,448},{4... | collective-permute-start | bytes 786440 | tf_op jit(solution)/shard_map/ppermute | solution.py:140
  123.2 19.6 %collective-permute-start.11 = (bf16[256,512]{0,1:T(8,128)(2,1)S(1)}, bf16[256,512]{0,1:T(8,128)(2,1)S(1)}, u32[]{:S(2)}, u32[]{:S(2)}) collective-permute-start(bf16[256,512]{0,1:T(8,128)(2,1)S(1)} %pad_maximum_fusion.1), channel_id=1, source_target_pairs={{0,128},{64,192},{128,0},{192,64},{256,384},{320,448},{384,256},{4... | collective-permute-start | bytes 786440 | tf_op jit(solution)/shard_map/ppermute | solution.py:140
  125.2 22.9 %collective-permute-start.12 = (bf16[256,512]{0,1:T(8,128)(2,1)S(1)}, bf16[256,512]{0,1:T(8,128)(2,1)S(1)}, u32[]{:S(2)}, u32[]{:S(2)}) collective-permute-start(bf16[256,512]{0,1:T(8,128)(2,1)S(1)} %pad_maximum_fusion.1), channel_id=1, source_target_pairs={{0,192},{64,128},{128,64},{192,0},{256,448},{320,384},{384,320},{4... | collective-permute-start | bytes 786440 | tf_op jit(solution)/shard_map/ppermute | solution.py:140
  151.7 56.6 %copy-start.1 = (f32[16,2]{0,1:T(2,128)S(1)}, f32[16,2]{0,1:T(2,128)}, u32[]{:S(2)}) copy-start(f32[16,2]{0,1:T(2,128)} %param.8) | copy-start | bytes 388

commit v3 on v2

--- a/solution.py
+++ b/solution.py
@@ -1,6 +1,8 @@
 import jax
 import jax.numpy as jnp
 from jax import lax
+from jax.experimental import pallas as pl
+from jax.experimental.pallas import tpu as pltpu
 from jax.sharding import Mesh, PartitionSpec as P
 
 AXES = ("zl", "y", "c", "zh", "x")
@@ -30,6 +32,65 @@
     earlier = index[None, :] < index[:, None]
     position = jnp.sum((same & earlier).astype(jnp.int32), axis=1)
     return (flat * capacity + position).reshape(expert_ids.shape)
+
+
+DEPTH = 768
+
+
+def gated_kernel(core_ref, rows_ref, g0, u0, g1, u1, out_ref, gate, up):
+    at = pl.program_id(0)
+
+    @pl.when(at == 0)
+    def _():
+        gate[...] = jnp.zeros_like(gate)
+        up[...] = jnp.zeros_like(up)
+
+    lhs = rows_ref[...]
+    w_g = jnp.concatenate([g0[...], g1[...]], axis=1)
+    w_u = jnp.concatenate([u0[...], u1[...]], axis=1)
+    gate[...] += jnp.dot(lhs, w_g, preferred_element_type=jnp.float32)
+    up[...] += jnp.dot(lhs, w_u, preferred_element_type=jnp.float32)
+
+    @pl.when(at == pl.num_programs(0) - 1)
+    def _():
+        g = gate[...]
+        value = (g / (1.0 + jnp.exp(-g)) * up[...]).astype(out_ref.dtype)
+        n = value.shape[1] // 2
+
+        @pl.when(core_ref[0] == 0)
+        def _():
+            out_ref[...] = value
+
+        @pl.when(core_ref[0] != 0)
+        def _():
+            out_ref[...] = jnp.concatenate([value[:, n:], value[:, :n]], axis=1)
+
+
+def gated(core, rows, g0, u0, g1, u1):
+    m, depth = rows.shape
+    units = g0.shape[1]
+    weight = pl.BlockSpec((DEPTH, units), lambda i, core: (i, 0))
+    return pl.pallas_call(
+        gated_kernel,
+        out_shape=jax.ShapeDtypeStruct((m, 2 * units), rows.dtype),
+        grid_spec=pltpu.PrefetchScalarGridSpec(
+            num_scalar_prefetch=1,
+            grid=(depth // DEPTH,),
+            in_specs=[pl.BlockSpec((m, DEPTH), lambda i, core: (0, i))] + [weight] * 4,
+            out_specs=pl.BlockSpec((m, 2 * units), lambda i, core: (0, 0)),
+            scratch_shapes=[
+                pltpu.VMEM((m, 2 * units), jnp.float32),
+                pltpu.VMEM((m, 2 * units), jnp.float32),
+            ],
+        ),
+        compiler_params=pltpu.CompilerParams(dimension_semantics=("arbitrary",)),
+        cost_estimate=pl.CostEstimate(
+            flops=2 * m * depth * units * 4,
+            transcendentals=m * units * 2,
+            bytes_accessed=depth * (m + 4 * units) * 2,
+        ),
+        name="gated",
+    )(core, rows, g0, u0, g1, u1)
 
 
 def per_device(tokens, expert_ids, gate_probs, w_gate, w_up, w_down_t):
@@ -114,11 +175,6 @@
     blocks = (piece, up1, dn1, jnp.concatenate([far_a, far_b], axis=0))
     first = lax.axis_index("c") == 0
 
-    def act(rows_in, w1, w2):
-        gate = jnp.dot(rows_in, w1, preferred_element_type=f32)
-        up = jnp.dot(rows_in, w2, preferred_element_type=f32)
-        return (jax.nn.silu(gate) * up).astype(bf16)
-
     def out(hidden, w):
         total = 0.0
         for k, h in enumerate(hidden):
@@ -130,18 +186,17 @@
             )
         return total.astype(bf16)
 
-    taken = jnp.concatenate(blocks, axis=0)
-    own, far = act(taken, gate_own, up_own), act(taken, gate_far, up_far)
-    hidden = jnp.concatenate(
-        [jnp.where(first, own, far), jnp.where(first, far, own)], axis=1
+    core = lax.axis_index("c").astype(jnp.int32).reshape(1)
+    hidden = gated(
+        core, jnp.concatenate(blocks, axis=0), gate_own, up_own, gate_far, up_far
     )
     other = lax.ppermute(hidden, "zl", flip(zl, 4))
     pair = jnp.concatenate([hidden, other], axis=1)
     pairs = [pair] + [lax.ppermute(pair, "zl", flip(zl, k)) for k in (1, 2, 3)]
-    own, far = out(pairs, down), out(pairs, down_far)
-    part = jnp.concatenate(
-        [jnp.where(first, own, far), jnp.where(first, far, own)], axis=1
-    )
+    both = jnp.concatenate(
+        [jnp.where(first, down, down_far), jnp.where(first, down_far, down)], axis=0
+    )
+    part = out(pairs, both)
     parts = [part[n * rows : (n + 1) * rows] for n in range(y)]
 
     part = jnp.stack([parts[0], parts[2], parts[3], parts[1]])
@@ -151,14 +206,23 @@
     part = lax.all_to_all(part, "y", 0, 0, tiled=True).astype(f32)
     result = ((part[0] + part[1]) + (part[2] + part[3])).astype(bf16)
 
-    result = lax.all_to_all(
-        result.reshape(zl, capacity, width), "zl", 0, 0, tiled=True
-    )
-    result = lax.all_to_all(result, ("zh", "x"), 0, 0, tiled=True)
+    result = jnp.broadcast_to(
+        result.reshape(1, zl, capacity * width), (zh, zl, capacity * width)
+    ).reshape(zh * zl, capacity, width)
+    result = lax.all_to_all(result, ("zh", "zl"), 0, 0, tiled=True)
+    result = result.reshape(zh, zl, capacity, width)
+    result = lax.dynamic_slice_in_dim(result, lax.axis_index("zh") * x, x, 1)
+    result = jnp.concatenate([result[h] for h in range(zh)], axis=1)
+    result = lax.all_to_all(result, "x", 0, 0, tiled=True)
     result, slot, gate_probs = lax.optimization_barrier((result, slot, gate_probs))
     result = result.reshape(experts * capacity, width)
 
     every = jnp.arange(experts * capacity, dtype=jnp.int32)
+    every = (
+        (every // capacity % zh) * (x * capacity)
+        + (every // (zh * capacity)) * capacity
+        + every % capacity
+    )
     mixed = 0.0
     for k in range(2):
         pick = (slot[:, k][:, None] == every[None, :]).astype(bf16)

time: 211 us -> 201 us (0.953)
  the two profiles are of different devices: /device:TPU:32 before, /device:TPU:2 now
where the time goes in v3:
time: 201 us; the launch traced here: 200 us
  starting transfers between devices  96.2 us (48%)
  waiting for transfers between devices  51.1 us (25%)
  local copies, waits for them, and re-layouts  20.3 us (10%)
  blocking collectives  14.5 us (7%)
  Pallas kernels  8.01 us (4%)
  other arithmetic  5.96 us (3%)
  matrix products  2.65 us (1%)
    all_to_all x1, starting transfers between devices, per_device(): result = lax.all_to_all(result, ('zh', 'zl'), 0, 0, tiled=True)  16.7 us
    all_to_all x1, waiting for transfers between devices, per_device(): result = lax.all_to_all(result, ('zh', 'zl'), 0, 0, tiled=True)  15.7 us
    all_to_all x1, starting transfers between devices, everyone(): lax.all_to_all(jnp.broadcast_to(value[None], (count,) + value.shape), axi...  15.2 us
    ppermute x3, starting transfers between devices, per_device(): pairs = [pair] + [lax.ppermute(pair, 'zl', flip(zl, k)) for k in (1, 2, 3)]  14.6 us
    unnamed x40, local copies, waits for them, and re-layouts  14.5 us
    all_to_all x1, blocking collectives, per_device(): part = lax.all_to_all(part, 'y', 0, 0, tiled=True).astype(f32)  14.5 us
    ppermute x3, starting transfers between devices, per_device(): moved = lax.ppermute(moved, 'y', step(y, k))  11.5 us
    ppermute x3, waiting for transfers between devices, per_device(): pairs = [pair] + [lax.ppermute(pair, 'zl', flip(zl, k)) for k in (1, 2, 3)]  10.4 us
  transfers between devices with their start and end apart: 18, of which 10 were waited for; matrix products, arithmetic and copies ran while one was open for 10% of the time, Pallas kernels for 4%

profile of v3, /device:TPU:2, one launch (start us, length us, event | category | flops | bytes accessed | tf_op | source)
XLA Modules:
  0.0 199.7 jit_solution(17223701580459040293)
XLA Ops:
  3.7 15.2 %all-to-all-start = ((bf16[16,16,896]{2,1,0:T(8,128)(2,1)}), bf16[16,16,896]{2,1,0:T(8,128)(2,1)S(1)}, u32[]{:S(2)}, u32[]{:S(2)}) async-start(bf16[16,16,896]{2,1,0:T(8,128)(2,1)} %broadcast_in_dim.14), calls=%async_computation | async-start | bytes 917504 | tf_op jit(solution)/shard_map/all_to_all | solution.py:22
  24.7 3.5 %collective-permute-start = (bf16[96,2048]{1,0:T(8,128)(2,1)}, bf16[96,2048]{1,0:T(8,128)(2,1)S(1)}, u32[]{:S(2)}, u32[]{:S(2)}) collective-permute-start(bf16[96,2048]{1,0:T(8,128)(2,1)} %get-tuple-element.27), channel_id=1, source_target_pairs={{0,16},{16,32},{32,48},{48,0},{1,17},{17,33},{33,49},{49,1},{2,18}... | collective-permute-start | bytes 1179656 | tf_op jit(solution)/shard_map/ppermute | solution.py:130
  28.2 4.8 %collective-permute-start.1 = (bf16[96,2048]{1,0:T(8,128)(2,1)}, bf16[96,2048]{1,0:T(8,128)(2,1)}, u32[]{:S(2)}, u32[]{:S(2)}) collective-permute-start(bf16[96,2048]{1,0:T(8,128)(2,1)} %get-tuple-element.26), channel_id=1, source_target_pairs={{0,32},{16,48},{32,0},{48,16},{1,33},{17,49},{33,1},{49,17},{2,34}... | collective-permute-start | bytes 1179656 | tf_op jit(solution)/shard_map/ppermute | solution.py:130
  33.0 3.3 %collective-permute-start.2 = (bf16[96,2048]{1,0:T(8,128)(2,1)}, bf16[96,2048]{1,0:T(8,128)(2,1)S(1)}, u32[]{:S(2)}, u32[]{:S(2)}) collective-permute-start(bf16[96,2048]{1,0:T(8,128)(2,1)} %get-tuple-element.25), channel_id=1, source_target_pairs={{0,48},{16,0},{32,16},{48,32},{1,49},{17,1},{33,17},{49,33},{2,50}... | collective-permute-start | bytes 1179656 | tf_op jit(solution)/shard_map/ppermute | solution.py:130
  41.2 4.6 %all-to-all-done = bf16[16,16,896]{2,1,0:T(8,128)(2,1)S(1)} async-done(((bf16[16,16,896]{2,1,0:T(8,128)(2,1)}), bf16[16,16,896]{2,1,0:T(8,128)(2,1)S(1)}, u32[]{:S(2)}, u32[]{:S(2)}) %all-to-all-start) | async-done | bytes 458784 | tf_op jit(solution)/shard_map/all_to_all | solution.py:22
  47.7 4.8 %all-to-all-start.1 = ((bf16[4,128,768]{2,1,0:T(8,128)(2,1)}), bf16[4,128,768]{2,1,0:T(8,128)(2,1)S(1)}, u32[]{:S(2)}, u32[]{:S(2)}) async-start(bf16[4,128,768]{2,1,0:T(8,128)(2,1)} %pad_maximum_fusion.2), calls=%async_computation.1 | async-start | bytes 1572864 | tf_op jit(solution)/shard_map/all_to_all | solution.py:161
  53.6 6.9 %all-to-all-done.1 = bf16[4,128,768]{2,1,0:T(8,128)(2,1)S(1)} async-done(((bf16[4,128,768]{2,1,0:T(8,128)(2,1)}), bf16[4,128,768]{2,1,0:T(8,128)(2,1)S(1)}, u32[]{:S(2)}, u32[]{:S(2)}) %all-to-all-start.1) | async-done | bytes 786464 | tf_op jit(solution)/shard_map/all_to_all | solution.py:161
  61.3 3.5 %collective-permute-start.5 = (bf16[64,6144]{1,0:T(8,128)(2,1)S(1)}, bf16[64,6144]{1,0:T(8,128)(2,1)S(1)}, u32[]{:S(2)}, u32[]{:S(2)}) collective-permute-start(bf16[64,6144]{1,0:T(8,128)(2,1)S(1)} %get-tuple-element.57), channel_id=1, source_target_pairs={{0,16},{16,32},{32,48},{48,0},{1,17},{17,33},{33,49},{49,1},{2,18}... | collective-permute-start | bytes 2359304 | tf_op jit(solution)/shard_map/ppermute | solution.py:170
  64.8 3.6 %collective-permute-start.6 = (bf16[64,6144]{1,0:T(8,128)(2,1)S(1)}, bf16[64,6144]{1,0:T(8,128)(2,1)S(1)}, u32[]{:S(2)}, u32[]{:S(2)}) collective-permute-start(bf16[64,6144]{1,0:T(8,128)(2,1)S(1)} %get-tuple-element.57), channel_id=1, source_target_pairs={{0,48},{16,0},{32,16},{48,32},{1,49},{17,1},{33,17},{49,33},{2,50}... | collective-permute-start | bytes 2359304 | tf_op jit(solution)/shard_map/ppermute | solution.py:171
  74.9 2.9 %collective-permute-done.5 = bf16[64,6144]{1,0:T(8,128)(2,1)S(1)} collective-permute-done((bf16[64,6144]{1,0:T(8,128)(2,1)S(1)}, bf16[64,6144]{1,0:T(8,128)(2,1)S(1)}, u32[]{:S(2)}, u32[]{:S(2)}) %collective-permute-start.5) | collective-permute-done | bytes 786464 | tf_op jit(solution)/shard_map/ppermute | solution.py:170
  79.8 5.1 %collective-permute-start.8 = (bf16[32,6144]{1,0:T(8,128)(2,1)S(1)}, bf16[32,6144]{1,0:T(8,128)(2,1)S(1)}, u32[]{:S(2)}, u32[]{:S(2)}) collective-permute-start(bf16[32,6144]{1,0:T(8,128)(2,1)S(1)} %slice.138), channel_id=1, source_target_pairs={{0,48},{16,0},{32,16},{48,32},{1,49},{17,1},{33,17},{49,33},{2,50}... | collective-permute-start | bytes 1179656 | tf_op jit(solution)/shard_map/ppermute | solution.py:174
  86.9 2.7 %collective-permute-done.7 = bf16[32,6144]{1,0:T(8,128)(2,1)S(1)} collective-permute-done((bf16[32,6144]{1,0:T(8,128)(2,1)S(1)}, bf16[32,6144]{1,0:T(8,128)(2,1)S(1)}, u32[]{:S(2)}, u32[]{:S(2)}) %collective-permute-start.7) | collective-permute-done | bytes 393248 | tf_op jit(solution)/shard_map/ppermute | solution.py:173
  91.6 8.0 %gated.1 = bf16[256,256]{1,0:T(8,128)(2,1)} custom-call(s32[1]{0:T(128)} %bitcast.core_ref, bf16[256,6144]{1,0:T(8,128)(2,1)} %constant_dynamic-update-slice_fusion.40.rows_ref, bf16[6144,128]{1,0:T(8,128)(2,1)} %bitcast.44.g0, bf16[6144,128]{1,0:T(8,128)(2,1)} %bitcast.45.u0, bf16[6144,128]{1,0:T(8,128)(2,1)} %collective-permute-done.3.g1, ...), custom_call_target="tpu_custom_call" | custom-call | flops 1610612736 | bytes 9437184 | tf_op jit(solution)/shard_map/gated/pallas_call | solution.py:73
  99.6 8.4 %collective-permute-start.9 = (bf16[256,256]{1,0:T(8,128)(2,1)}, bf16[256,256]{1,0:T(8,128)(2,1)S(1)}, u32[]{:S(2)}, u32[]{:S(2)}) collective-permute-start(bf16[256,256]{1,0:T(8,128)(2,1)} %gated.1), channel_id=1, source_target_pairs={{0,256},{64,320},{128,384},{192,448},{256,0},{320,64},{384,128},{4... | collective-permute-start | bytes 393224 | tf_op jit(solution)/shard_map/ppermute | solution.py:193
  108.0 3.1 %collective-permute-done.9 = bf16[256,256]{1,0:T(8,128)(2,1)S(1)} collective-permute-done((bf16[256,256]{1,0:T(8,128)(2,1)}, bf16[256,256]{1,0:T(8,128)(2,1)S(1)}, u32[]{:S(2)}, u32[]{:S(2)}) %collective-permute-start.9) | collective-permute-done | bytes 131104 | tf_op jit(solution)/shard_map/ppermute | solution.py:193
  112.1 8.4 %collective-permute-start.11 = (bf16[256,512]{1,0:T(8,128)(2,1)S(1)}, bf16[256,512]{1,0:T(8,128)(2,1)S(1)}, u32[]{:S(2)}, u32[]{:S(2)}) collective-permute-start(bf16[256,512]{1,0:T(8,128)(2,1)S(1)} %pad_maximum_fusion.3), channel_id=1, source_target_pairs={{0,64},{64,0},{128,192},{192,128},{256,320},{320,256},{384,448},{4... | collective-permute-start | bytes 786440 | tf_op jit(solution)/shard_map/ppermute | solution.py:195
  120.4 3.4 %collective-permute-start.12 = (bf16[256,512]{1,0:T(8,128)(2,1)S(1)}, bf16[256,512]{1,0:T(8,128)(2,1)S(1)}, u32[]{:S(2)}, u32[]{:S(2)}) collective-permute-start(bf16[256,512]{1,0:T(8,128)(2,1)S(1)} %pad_maximum_fusion.3), channel_id=1, source_target_pairs={{0,128},{64,192},{128,0},{192,64},{256,384},{320,448},{384,256},{4... | collective-permute-start | bytes 786440 | tf_op jit(solution)/shard_map/ppermute | solution.py:195
  123.8 2.8 %collective-permute-start.13 = (bf16[256,512]{1,0:T(8,128)(2,1)S(1)}, bf16[256,512]{1,0:T(8,128)(2,1)S(1)}, u32[]{:S(2)}, u32[]{:S(2)}) collective-permute-start(bf16[256,512]{1,0:T(8,128)(2,1)S(1)} %pad_maximum_fusion.3), channel_id=1, source_target_pairs={{0,192},{64,128},{128,64},{192,0},{256,448},{320,384},{384,320},{4... | collective-permute-start | bytes 786440 | tf_op jit(solution)/shard_map/ppermute | solution.py:195
  129.6 9.4 %collective-permute-done.12 = bf16[256,512]{1,0:T(8,128)(2,1)S(1)} collective-permute-done((bf16[256,512]{1,0:T(8,128)(2,1)S(1)}, bf16[256,512]{1,0:T(8,128)(2,1)S(1)}, u32[]{:S(2)}, u32[]{:S(2)}) %collective-permute-start.12) | collective-permute-done | bytes 262176 | tf_op jit(solution)/shard_map/ppermute | solution.py:195
  141.0 14.5 %all_to_all.25 = bf16[4,64,768]{2,1,0:T(8,128)(2,1)S(1)} all-to-all(bf16[4,64,768]{2,1,0:T(8,128)(2,1)S(1)} %constant_dynamic-slice_fusion), channel_id=1, replica_groups=mesh['zl'=8,'y'=4,'c'=2,'zh'=2,'x'=4] {'y'}, dimensions={0} | all-to-all | bytes 786432 | tf_op jit(solution)/shard_map/all_to_all | solution.py:206
  156.4 16.7 %all-to-all-start.3 = ((bf16[16,8,768]{2,1,0:T(8,128)(2,1)}), bf16[16,8,768]{2,1,0:T(8,128)(2,1)S(1)}, u32[]{:S(2)}, u32[]{:S(2)}) async-start(bf16[16,8,768]{2,1,0:T(8,128)(2,1)} %bitcast.69), calls=%async_computation.3 | async-start | bytes 393216 | tf_op jit(solution)/shard_map/all_to_all | solution.py:212
  173.1 15.7 %all-to-all-done.3 = bf16[16,8,768]{2,1,0:T(8,128)(2,1)S(1)} async-done(((bf16[16,8,768]{2,1,0:T(8,128)(2,1)}), bf16[16,8,768]{2,1,0:T(8,128)(2,1)S(1)}, u32[]{:S(2)}, u32[]{:S(2)}) %all-to-all-start.3) | async-done | bytes 196640 | tf_op jit(solution)/shard_map/all_to_all | solution.py:212
  189.4 4.7 %all-to-all-start.4 = ((bf16[4,16,768]{2,1,0:T(8,128)(2,1)}), bf16[4,16,768]{2,1,0:T(8,128)(2,1)S(1)}, u32[]{:S(2)}, u32[]{:S(2)}) async-start(bf16[4,16,768]{2,1,0:T(8,128)(2,1)} %pad_maximum_fusion.4), calls=%async_computation.4 | async-start | bytes 196608 | tf_op jit(solution)/shard_map/all_to_all | solution.py:216
  194.1 4.3 %all-to-all-done.4 = bf16[4,16,768]{2,1,0:T(8,128)(2,1)S(1)} async-done(((bf16[4,16,768]{2,1,0:T(8,128)(2,1)}), bf16[4,16,768]{2,1,0:T(8,128)(2,1)S(1)}, u32[]{:S(2)}, u32[]{:S(2)}) %all-to-all-start.4) | async-done | bytes 98336 | tf_op jit(solution)/shard_map/all_to_all | solution.py:216
  (104 shorter events, 38.5 us)
Async XLA Ops:
  0.0 19.2 %copy-start = (bf16[1,96,8192]{2,1,0:T(8,128)(2,1)S(1)}, bf16[1,96,8192]{2,1,0:T(8,128)(2,1)}, u32[]{:S(2)}) copy-start(bf16[1,96,8192]{2,1,0:T(8,128)(2,1)} %param.11) | copy-start | bytes 4718596
  3.7 42.2 %all-to-all-start = ((bf16[16,16,896]{2,1,0:T(8,128)(2,1)}), bf16[16,16,896]{2,1,0:T(8,128)(2,1)S(1)}, u32[]{:S(2)}, u32[]{:S(2)}) async-start(bf16[16,16,896]{2,1,0:T(8,128)(2,1)} %broadcast_in_dim.14), calls=%async_computation | async-start | bytes 917504 | tf_op jit(solution)/shard_map/all_to_all | solution.py:22
  24.7 16.4 %collective-permute-start = (bf16[96,2048]{1,0:T(8,128)(2,1)}, bf16[96,2048]{1,0:T(8,128)(2,1)S(1)}, u32[]{:S(2)}, u32[]{:S(2)}) collective-permute-start(bf16[96,2048]{1,0:T(8,128)(2,1)} %get-tuple-element.27), channel_id=1, source_target_pairs={{0,16},{16,32},{32,48},{48,0},{1,17},{17,33},{33,49},{49,1},{2,18}... | collective-permute-start | bytes 1179656 | tf_op jit(solution)/shard_map/ppermute | solution.py:130
  28.2 24.3 %collective-permute-start.1 = (bf16[96,2048]{1,0:T(8,128)(2,1)}, bf16[96,2048]{1,0:T(8,128)(2,1)}, u32[]{:S(2)}, u32[]{:S(2)}) collective-permute-start(bf16[96,2048]{1,0:T(8,128)(2,1)} %get-tuple-element.26), channel_id=1, source_target_pairs={{0,32},{16,48},{32,0},{48,16},{1,33},{17,49},{33,1},{49,17},{2,34}... | collective-permute-start | bytes 1179656 | tf_op jit(solution)/shard_map/ppermute | solution.py:130
  33.0 20.5 %collective-permute-start.2 = (bf16[96,2048]{1,0:T(8,128)(2,1)}, bf16[96,2048]{1,0:T(8,128)(2,1)S(1)}, u32[]{:S(2)}, u32[]{:S(2)}) collective-permute-start(bf16[96,2048]{1,0:T(8,128)(2,1)} %get-tuple-element.25), channel_id=1, source_target_pairs={{0,48},{16,0},{32,16},{48,32},{1,49},{17,1},{33,17},{49,33},{2,50}... | collective-permute-start | bytes 1179656 | tf_op jit(solution)/shard_map/ppermute | solution.py:130
  36.3 17.3 %collective-permute-start.3 = (bf16[6144,128]{1,0:T(8,128)(2,1)}, bf16[6144,128]{1,0:T(8,128)(2,1)}, u32[]{:S(2)}, u32[]{:S(2)}) collective-permute-start(bf16[6144,128]{1,0:T(8,128)(2,1)} %bitcast.44.g0), channel_id=1, source_target_pairs={{0,8},{8,0},{1,9},{9,1},{2,10},{10,2},{3,11},{11,3},{4,12},{12,4},... | collective-permute-start | bytes 4718600 | tf_op jit(solution)/shard_map/ppermute | solution.py:106
  38.2 15.4 %collective-permute-start.4 = (bf16[6144,128]{1,0:T(8,128)(2,1)}, bf16[6144,128]{1,0:T(8,128)(2,1)}, u32[]{:S(2)}, u32[]{:S(2)}) collective-permute-start(bf16[6144,128]{1,0:T(8,128)(2,1)} %bitcast.45.u0), channel_id=1, source_target_pairs={{0,8},{8,0},{1,9},{9,1},{2,10},{10,2},{3,11},{11,3},{4,12},{12,4},... | collective-permute-start | bytes 4718600 | tf_op jit(solution)/shard_map/ppermute | solution.py:107
  47.7 12.9 %all-to-all-start.1 = ((bf16[4,128,768]{2,1,0:T(8,128)(2,1)}), bf16[4,128,768]{2,1,0:T(8,128)(2,1)S(1)}, u32[]{:S(2)}, u32[]{:S(2)}) async-start(bf16[4,128,768]{2,1,0:T(8,128)(2,1)} %pad_maximum_fusion.2), calls=%async_computation.1 | async-start | bytes 1572864 | tf_op jit(solution)/shard_map/all_to_all | solution.py:161
  61.3 16.5 %collective-permute-start.5 = (bf16[64,6144]{1,0:T(8,128)(2,1)S(1)}, bf16[64,6144]{1,0:T(8,128)(2,1)S(1)}, u32[]{:S(2)}, u32[]{:S(2)}) collective-permute-start(bf16[64,6144]{1,0:T(8,128)(2,1)S(1)} %get-tuple-element.57), channel_id=1, source_target_pairs={{0,16},{16,32},{32,48},{48,0},{1,17},{17,33},{33,49},{49,1},{2,18}... | collective-permute-start | bytes 2359304 | tf_op jit(solution)/shard_map/ppermute | solution.py:170
  64.8 15.0 %collective-permute-start.6 = (bf16[64,6144]{1,0:T(8,128)(2,1)S(1)}, bf16[64,6144]{1,0:T(8,128)(2,1)S(1)}, u32[]{:S(2)}, u32[]{:S(2)}) collective-permute-start(bf16[64,6144]{1,0:T(8,128)(2,1)S(1)} %get-tuple-element.57), channel_id=1, source_target_pairs={{0,48},{16,0},{32,16},{48,32},{1,49},{17,1},{33,17},{49,33},{2,50}... | collective-permute-start | bytes 2359304 | tf_op jit(solution)/shard_map/ppermute | solution.py:171
  71.0 55.6 %collective-permute-start.10 = (bf16[384,2048]{1,0:T(8,128)(2,1)S(1)}, bf16[384,2048]{1,0:T(8,128)(2,1)}, u32[]{:S(2)}, u32[]{:S(2)}) collective-permute-start(bf16[384,2048]{1,0:T(8,128)(2,1)S(1)} %bitcast.158), channel_id=1, source_target_pairs={{0,8},{8,0},{1,9},{9,1},{2,10},{10,2},{3,11},{11,3},{4,12},{12,4},... | collective-permute-start | bytes 4718600 | tf_op jit(solution)/shard_map/ppermute | solution.py:169
  77.8 11.7 %collective-permute-start.7 = (bf16[32,6144]{1,0:T(8,128)(2,1)S(1)}, bf16[32,6144]{1,0:T(8,128)(2,1)S(1)}, u32[]{:S(2)}, u32[]{:S(2)}) collective-permute-start(bf16[32,6144]{1,0:T(8,128)(2,1)S(1)} %slice.137), channel_id=1, source_target_pairs={{0,16},{16,32},{32,48},{48,0},{1,17},{17,33},{33,49},{49,1},{2,18}... | collective-permute-start | bytes 1179656 | tf_op jit(solution)/shard_map/ppermute | solution.py:173
  79.8 11.0 %collective-permute-start.8 = (bf16[32,6144]{1,0:T(8,128)(2,1)S(1)}, bf16[32,6144]{1,0:T(8,128)(2,1)S(1)}, u32[]{:S(2)}, u32[]{:S(2)}) collective-permute-start(bf16[32,6144]{1,0:T(8,128)(2,1)S(1)} %slice.138), channel_id=1, source_target_pairs={{0,48},{16,0},{32,16},{48,32},{1,49},{17,1},{33,17},{49,33},{2,50}... | collective-permute-start | bytes 1179656 | tf_op jit(solution)/shard_map/ppermute | solution.py:174
  99.6 11.5 %collective-permute-start.9 = (bf16[256,256]{1,0:T(8,128)(2,1)}, bf16[256,256]{1,0:T(8,128)(2,1)S(1)}, u32[]{:S(2)}, u32[]{:S(2)}) collective-permute-start(bf16[256,256]{1,0:T(8,128)(2,1)} %gated.1), channel_id=1, source_target_pairs={{0,256},{64,320},{128,384},{192,448},{256,0},{320,64},{384,128},{4... | collective-permute-start | bytes 393224 | tf_op jit(solution)/shard_map/ppermute | solution.py:193
  112.1 17.2 %collective-permute-start.11 = (bf16[256,512]{1,0:T(8,128)(2,1)S(1)}, bf16[256,512]{1,0:T(8,128)(2,1)S(1)}, u32[]{:S(2)}, u32[]{:S(2)}) collective-permute-start(bf16[256,512]{1,0:T(8,128)(2,1)S(1)} %pad_maximum_fusion.3), channel_id=1, source_target_pairs={{0,64},{64,0},{128,192},{192,128},{256,320},{320,256},{384,448},{4... | collective-permute-start | bytes 786440 | tf_op jit(solution)/shard_map/ppermute | solution.py:195
  120.4 18.6 %collective-permute-start.12 = (bf16[256,512]{1,0:T(8,128)(2,1)S(1)}, bf16[256,512]{1,0:T(8,128)(2,1)S(1)}, u32[]{:S(2)}, u32[]{:S(2)}) collective-permute-start(bf16[256,512]{1,0:T(8,128)(2,1)S(1)} %pad_maximum_fusion.3), channel_id=1, source_target_pairs={{0,128},{64,192},{128,0},{192,64},{256,384},{320,448},{384,256},{4... | collective-permute-start | bytes 786440 | tf_op jit(solution)/shard_map/ppermute | solution.py:195
  123.8 15.7 %collective-permute-start.13 = (bf16[256,512]{1,0:T(8,128)(2,1)S(1)}, bf16[256,512]{1,0:T(8,128)(2,1)S(1)}, u32[]{:S(2)}, u32[]{:S(2)}) collective-permute-start(bf16[256,512]{1,0:T(8,128)(2,1)S(1)} %pad_maximum_fusion.3), channel_id=1, source_target_pairs={{0,192},{64,128},{128,64},{192,0},{256,448},{320,384},{384,320},{4... | collective-permute-start | bytes 786440 | tf_op jit(solution)/shard_map/ppermute | solution.py:195
  139.5 0.9 copy-start.1
  155.5 42.9 %copy-start.2 = (f32[16,2]{0,1:T(2,128)S(1)}, f32[16,2]{0,1:T(2,128)}, u32[]{:S(2)}) copy-start(f32[16,2]{0,1:T(2,128)} %param.8) | copy-start | bytes 388
  156.4 32.3 %all-to-all-start.3 = ((bf16[16,8,768]{2,1,0:T(8,128)(2,1)}), bf16[16,8,768]{2,1,0:T(8,128)(2,1)S(1)}, u32[]{:S(2)}, u32[]{:S(2)}) async-start(bf16[16,8,768]{2,1,0:T(8,128)(2,1)} %bitcast.69), calls=%async_computation.3 | async-start | bytes 393216 | tf_op jit(solution)/shard_map/all_to_all | solution.py:212
  189.4 9.1 %all-to-all-start.4 = ((bf16[4,16,768]{2,1,0:T(8,128)(2,1)}), bf16[4,16,768]{2,1,0:T(8,128)(2,1)S(1)}, u32[]{:S(2)}, u32[]{:S(2)}) async-start(bf16[4,16,768]{2,1,0:T(8,128)(2,1)} %pad_maximum_fusion.4), calls=%async_computation.4 | async-start | bytes 196608 | tf_op jit(solution)/shard_map/all_to_all | solution.py:216

commit v4 on v3

--- a/solution.py
+++ b/solution.py
@@ -34,7 +34,7 @@
     return (flat * capacity + position).reshape(expert_ids.shape)
 
 
-DEPTH = 768
+DEPTH = 2048
 
 
 def gated_kernel(core_ref, rows_ref, g0, u0, g1, u1, out_ref, gate, up):
@@ -107,7 +107,7 @@
     up_far = lax.ppermute(up_own, "c", SWAP)
     features = w_down_t.shape[1]
     z_here = lax.axis_index("zl")
-    order = [q ^ k for k in range(4) for q in (0, 4)]
+    order = range(zl)
     span = c * units
     y_here = lax.axis_index("y")
 
@@ -172,7 +172,7 @@
     half = rows // 2
     far_a = lax.ppermute(up1[:half], "y", step(y, 1))
     far_b = lax.ppermute(dn1[half:], "y", step(y, -1))
-    blocks = (piece, up1, dn1, jnp.concatenate([far_a, far_b], axis=0))
+    blocks = (piece, up1, dn1, far_a, far_b)
     first = lax.axis_index("c") == 0
 
     def out(hidden, w):
@@ -180,7 +180,7 @@
         for k, h in enumerate(hidden):
             total = total + lax.dot_general(
                 h,
-                w[:, k * 2 * span : (k + 1) * 2 * span],
+                w[:, k * span : (k + 1) * span],
                 (((1,), (1,)), ((), ())),
                 preferred_element_type=f32,
             )
@@ -191,8 +191,9 @@
         core, jnp.concatenate(blocks, axis=0), gate_own, up_own, gate_far, up_far
     )
     other = lax.ppermute(hidden, "zl", flip(zl, 4))
-    pair = jnp.concatenate([hidden, other], axis=1)
-    pairs = [pair] + [lax.ppermute(pair, "zl", flip(zl, k)) for k in (1, 2, 3)]
+    near = [lax.ppermute(hidden, "zl", flip(zl, k)) for k in (1, 2, 3)]
+    distant = [lax.ppermute(other, "zl", flip(zl, k)) for k in (1, 2, 3)]
+    pairs = [hidden, *near, other, *distant]
     both = jnp.concatenate(
         [jnp.where(first, down, down_far), jnp.where(first, down_far, down)], axis=0
     )

time: 201 us -> 186 us (0.925)
  the two profiles are of different devices: /device:TPU:2 before, /device:TPU:32 now
where the time goes in v4:
time: 186 us; the launch traced here: 185 us
  starting transfers between devices  95.9 us (52%)
  waiting for transfers between devices  42.3 us (23%)
  local copies, waits for them, and re-layouts  19.8 us (11%)
  blocking collectives  12.1 us (7%)
  Pallas kernels  5.93 us (3%)
  other arithmetic  5.04 us (3%)
  matrix products  3.46 us (2%)
    all_to_all x1, starting transfers between devices, everyone(): lax.all_to_all(jnp.broadcast_to(value[None], (count,) + value.shape), axi...  15.2 us
    unnamed x40, local copies, waits for them, and re-layouts  14 us
    all_to_all x1, waiting for transfers between devices, per_device(): result = lax.all_to_all(result, ('zh', 'zl'), 0, 0, tiled=True)  13.4 us
    all_to_all x1, blocking collectives, per_device(): part = lax.all_to_all(part, 'y', 0, 0, tiled=True).astype(f32)  12.1 us
    ppermute x3, starting transfers between devices, per_device(): moved = lax.ppermute(moved, 'y', step(y, k))  11.5 us
    ppermute x3, starting transfers between devices, per_device(): distant = [lax.ppermute(other, 'zl', flip(zl, k)) for k in (1, 2, 3)]  11 us
    all_to_all x1, starting transfers between devices, per_device(): result = lax.all_to_all(result, ('zh', 'zl'), 0, 0, tiled=True)  10.9 us
    ppermute x3, starting transfers between devices, per_device(): near = [lax.ppermute(hidden, 'zl', flip(zl, k)) for k in (1, 2, 3)]  10.8 us
  transfers between devices with their start and end apart: 21, of which 9 were waited for; matrix products, arithmetic and copies ran while one was open for 11% of the time, Pallas kernels for 3%

profile of v4, /device:TPU:32, one launch (start us, length us, event | category | flops | bytes accessed | tf_op | source)
XLA Modules:
  0.0 185.3 jit_solution(15382898046849818788)
XLA Ops:
  3.7 15.2 %all-to-all-start = ((bf16[16,16,896]{2,1,0:T(8,128)(2,1)}), bf16[16,16,896]{2,1,0:T(8,128)(2,1)S(1)}, u32[]{:S(2)}, u32[]{:S(2)}) async-start(bf16[16,16,896]{2,1,0:T(8,128)(2,1)} %broadcast_in_dim.14), calls=%async_computation | async-start | bytes 917504 | tf_op jit(solution)/shard_map/all_to_all | solution.py:22
  24.4 3.5 %collective-permute-start = (bf16[96,2048]{1,0:T(8,128)(2,1)}, bf16[96,2048]{1,0:T(8,128)(2,1)S(1)}, u32[]{:S(2)}, u32[]{:S(2)}) collective-permute-start(bf16[96,2048]{1,0:T(8,128)(2,1)} %get-tuple-element.27), channel_id=1, source_target_pairs={{0,16},{16,32},{32,48},{48,0},{1,17},{17,33},{33,49},{49,1},{2,18}... | collective-permute-start | bytes 1179656 | tf_op jit(solution)/shard_map/ppermute | solution.py:130
  27.9 4.8 %collective-permute-start.1 = (bf16[96,2048]{1,0:T(8,128)(2,1)}, bf16[96,2048]{1,0:T(8,128)(2,1)}, u32[]{:S(2)}, u32[]{:S(2)}) collective-permute-start(bf16[96,2048]{1,0:T(8,128)(2,1)} %get-tuple-element.26), channel_id=1, source_target_pairs={{0,32},{16,48},{32,0},{48,16},{1,33},{17,49},{33,1},{49,17},{2,34}... | collective-permute-start | bytes 1179656 | tf_op jit(solution)/shard_map/ppermute | solution.py:130
  32.7 3.3 %collective-permute-start.2 = (bf16[96,2048]{1,0:T(8,128)(2,1)}, bf16[96,2048]{1,0:T(8,128)(2,1)S(1)}, u32[]{:S(2)}, u32[]{:S(2)}) collective-permute-start(bf16[96,2048]{1,0:T(8,128)(2,1)} %get-tuple-element.25), channel_id=1, source_target_pairs={{0,48},{16,0},{32,16},{48,32},{1,49},{17,1},{33,17},{49,33},{2,50}... | collective-permute-start | bytes 1179656 | tf_op jit(solution)/shard_map/ppermute | solution.py:130
  37.9 2.4 %collective-permute-start.4 = (bf16[6144,128]{1,0:T(8,128)(2,1)}, bf16[6144,128]{1,0:T(8,128)(2,1)}, u32[]{:S(2)}, u32[]{:S(2)}) collective-permute-start(bf16[6144,128]{1,0:T(8,128)(2,1)} %bitcast.45.u0), channel_id=1, source_target_pairs={{0,8},{8,0},{1,9},{9,1},{2,10},{10,2},{3,11},{11,3},{4,12},{12,4},... | collective-permute-start | bytes 4718600 | tf_op jit(solution)/shard_map/ppermute | solution.py:107
  44.8 4.3 %all-to-all-start.1 = ((bf16[4,128,768]{2,1,0:T(8,128)(2,1)}), bf16[4,128,768]{2,1,0:T(8,128)(2,1)S(1)}, u32[]{:S(2)}, u32[]{:S(2)}) async-start(bf16[4,128,768]{2,1,0:T(8,128)(2,1)} %pad_maximum_fusion), calls=%async_computation.1 | async-start | bytes 1572864 | tf_op jit(solution)/shard_map/all_to_all | solution.py:161
  50.2 9.3 %all-to-all-done.1 = bf16[4,128,768]{2,1,0:T(8,128)(2,1)S(1)} async-done(((bf16[4,128,768]{2,1,0:T(8,128)(2,1)}), bf16[4,128,768]{2,1,0:T(8,128)(2,1)S(1)}, u32[]{:S(2)}, u32[]{:S(2)}) %all-to-all-start.1) | async-done | bytes 786464 | tf_op jit(solution)/shard_map/all_to_all | solution.py:161
  60.3 3.5 %collective-permute-start.5 = (bf16[64,6144]{1,0:T(8,128)(2,1)S(1)}, bf16[64,6144]{1,0:T(8,128)(2,1)S(1)}, u32[]{:S(2)}, u32[]{:S(2)}) collective-permute-start(bf16[64,6144]{1,0:T(8,128)(2,1)S(1)} %get-tuple-element.57), channel_id=1, source_target_pairs={{0,16},{16,32},{32,48},{48,0},{1,17},{17,33},{33,49},{49,1},{2,18}... | collective-permute-start | bytes 2359304 | tf_op jit(solution)/shard_map/ppermute | solution.py:170
  63.8 3.6 %collective-permute-start.6 = (bf16[64,6144]{1,0:T(8,128)(2,1)S(1)}, bf16[64,6144]{1,0:T(8,128)(2,1)S(1)}, u32[]{:S(2)}, u32[]{:S(2)}) collective-permute-start(bf16[64,6144]{1,0:T(8,128)(2,1)S(1)} %get-tuple-element.57), channel_id=1, source_target_pairs={{0,48},{16,0},{32,16},{48,32},{1,49},{17,1},{33,17},{49,33},{2,50}... | collective-permute-start | bytes 2359304 | tf_op jit(solution)/shard_map/ppermute | solution.py:171
  73.9 5.6 %collective-permute-done.5 = bf16[64,6144]{1,0:T(8,128)(2,1)S(1)} collective-permute-done((bf16[64,6144]{1,0:T(8,128)(2,1)S(1)}, bf16[64,6144]{1,0:T(8,128)(2,1)S(1)}, u32[]{:S(2)}, u32[]{:S(2)}) %collective-permute-start.5) | collective-permute-done | bytes 786464 | tf_op jit(solution)/shard_map/ppermute | solution.py:170
  79.5 2.2 %collective-permute-start.7 = (bf16[32,6144]{1,0:T(8,128)(2,1)S(1)}, bf16[32,6144]{1,0:T(8,128)(2,1)S(1)}, u32[]{:S(2)}, u32[]{:S(2)}) collective-permute-start(bf16[32,6144]{1,0:T(8,128)(2,1)S(1)} %slice.153), channel_id=1, source_target_pairs={{0,16},{16,32},{32,48},{48,0},{1,17},{17,33},{33,49},{49,1},{2,18}... | collective-permute-start | bytes 1179656 | tf_op jit(solution)/shard_map/ppermute | solution.py:173
  81.8 4.8 %collective-permute-start.8 = (bf16[32,6144]{1,0:T(8,128)(2,1)S(1)}, bf16[32,6144]{1,0:T(8,128)(2,1)S(1)}, u32[]{:S(2)}, u32[]{:S(2)}) collective-permute-start(bf16[32,6144]{1,0:T(8,128)(2,1)S(1)} %slice.154), channel_id=1, source_target_pairs={{0,48},{16,0},{32,16},{48,32},{1,49},{17,1},{33,17},{49,33},{2,50}... | collective-permute-start | bytes 1179656 | tf_op jit(solution)/shard_map/ppermute | solution.py:174
  92.7 5.9 %gated.1 = bf16[256,256]{1,0:T(8,128)(2,1)} custom-call(s32[1]{0:T(128)} %bitcast.core_ref, bf16[256,6144]{1,0:T(8,128)(2,1)} %constant_dynamic-update-slice_fusion.40.rows_ref, bf16[6144,128]{1,0:T(8,128)(2,1)} %bitcast.44.g0, bf16[6144,128]{1,0:T(8,128)(2,1)} %bitcast.45.u0, bf16[6144,128]{1,0:T(8,128)(2,1)} %collective-permute-done.3.g1, ...), custom_call_target="tpu_custom_call" | custom-call | flops 1610612736 | bytes 9437184 | tf_op jit(solution)/shard_map/gated/pallas_call | solution.py:73
  98.6 8.5 %collective-permute-start.13 = (bf16[256,256]{1,0:T(8,128)(2,1)}, bf16[256,256]{1,0:T(8,128)(2,1)S(1)}, u32[]{:S(2)}, u32[]{:S(2)}) collective-permute-start(bf16[256,256]{1,0:T(8,128)(2,1)} %gated.1), channel_id=1, source_target_pairs={{0,256},{64,320},{128,384},{192,448},{256,0},{320,64},{384,128},{4... | collective-permute-start | bytes 393224 | tf_op jit(solution)/shard_map/ppermute | solution.py:193
  109.1 6.5 %collective-permute-start.11 = (bf16[256,256]{1,0:T(8,128)(2,1)}, bf16[256,256]{1,0:T(8,128)(2,1)S(1)}, u32[]{:S(2)}, u32[]{:S(2)}) collective-permute-start(bf16[256,256]{1,0:T(8,128)(2,1)} %gated.1), channel_id=1, source_target_pairs={{0,128},{64,192},{128,0},{192,64},{256,384},{320,448},{384,256},{4... | collective-permute-start | bytes 393224 | tf_op jit(solution)/shard_map/ppermute | solution.py:194
  115.6 2.5 %collective-permute-start.12 = (bf16[256,256]{1,0:T(8,128)(2,1)}, bf16[256,256]{1,0:T(8,128)(2,1)S(1)}, u32[]{:S(2)}, u32[]{:S(2)}) collective-permute-start(bf16[256,256]{1,0:T(8,128)(2,1)} %gated.1), channel_id=1, source_target_pairs={{0,192},{64,128},{128,64},{192,0},{256,448},{320,384},{384,320},{4... | collective-permute-start | bytes 393224 | tf_op jit(solution)/shard_map/ppermute | solution.py:194
  118.1 5.7 %collective-permute-start.15 = (bf16[256,256]{1,0:T(8,128)(2,1)S(1)}, bf16[256,256]{1,0:T(8,128)(2,1)S(1)}, u32[]{:S(2)}, u32[]{:S(2)}) collective-permute-start(bf16[256,256]{1,0:T(8,128)(2,1)S(1)} %collective-permute-done.13), channel_id=1, source_target_pairs={{0,128},{64,192},{128,0},{192,64},{256,384},{320,448},{384,256},{4... | collective-permute-start | bytes 393224 | tf_op jit(solution)/shard_map/ppermute | solution.py:195
  127.7 3.4 %collective-permute-start.14 = (bf16[256,256]{1,0:T(8,128)(2,1)S(1)}, bf16[256,256]{1,0:T(8,128)(2,1)S(1)}, u32[]{:S(2)}, u32[]{:S(2)}) collective-permute-start(bf16[256,256]{1,0:T(8,128)(2,1)S(1)} %collective-permute-done.13), channel_id=1, source_target_pairs={{0,64},{64,0},{128,192},{192,128},{256,320},{320,256},{384,448},{4... | collective-permute-start | bytes 393224 | tf_op jit(solution)/shard_map/ppermute | solution.py:195
  133.9 2.3 %collective-permute-done.16 = bf16[256,256]{1,0:T(8,128)(2,1)S(1)} collective-permute-done((bf16[256,256]{1,0:T(8,128)(2,1)S(1)}, bf16[256,256]{1,0:T(8,128)(2,1)S(1)}, u32[]{:S(2)}, u32[]{:S(2)}) %collective-permute-start.16) | collective-permute-done | bytes 131104 | tf_op jit(solution)/shard_map/ppermute | solution.py:195
  137.0 12.1 %all_to_all.25 = bf16[4,64,768]{2,1,0:T(8,128)(2,1)S(1)} all-to-all(bf16[4,64,768]{2,1,0:T(8,128)(2,1)S(1)} %constant_dynamic-slice_fusion), channel_id=1, replica_groups=mesh['zl'=8,'y'=4,'c'=2,'zh'=2,'x'=4] {'y'}, dimensions={0} | all-to-all | bytes 786432 | tf_op jit(solution)/shard_map/all_to_all | solution.py:207
  150.1 10.9 %all-to-all-start.3 = ((bf16[16,8,768]{2,1,0:T(8,128)(2,1)}), bf16[16,8,768]{2,1,0:T(8,128)(2,1)S(1)}, u32[]{:S(2)}, u32[]{:S(2)}) async-start(bf16[16,8,768]{2,1,0:T(8,128)(2,1)} %bitcast.69), calls=%async_computation.3 | async-start | bytes 393216 | tf_op jit(solution)/shard_map/all_to_all | solution.py:213
  160.9 13.4 %all-to-all-done.3 = bf16[16,8,768]{2,1,0:T(8,128)(2,1)S(1)} async-done(((bf16[16,8,768]{2,1,0:T(8,128)(2,1)}), bf16[16,8,768]{2,1,0:T(8,128)(2,1)S(1)}, u32[]{:S(2)}, u32[]{:S(2)}) %all-to-all-start.3) | async-done | bytes 196640 | tf_op jit(solution)/shard_map/all_to_all | solution.py:213
  175.0 3.3 %all-to-all-start.4 = ((bf16[4,16,768]{2,1,0:T(8,128)(2,1)}), bf16[4,16,768]{2,1,0:T(8,128)(2,1)S(1)}, u32[]{:S(2)}, u32[]{:S(2)}) async-start(bf16[4,16,768]{2,1,0:T(8,128)(2,1)} %pad_maximum_fusion.3), calls=%async_computation.4 | async-start | bytes 196608 | tf_op jit(solution)/shard_map/all_to_all | solution.py:217
  178.3 5.8 %all-to-all-done.4 = bf16[4,16,768]{2,1,0:T(8,128)(2,1)S(1)} async-done(((bf16[4,16,768]{2,1,0:T(8,128)(2,1)}), bf16[4,16,768]{2,1,0:T(8,128)(2,1)S(1)}, u32[]{:S(2)}, u32[]{:S(2)}) %all-to-all-start.4) | async-done | bytes 98336 | tf_op jit(solution)/shard_map/all_to_all | solution.py:217
  (113 shorter events, 41.9 us)
Async XLA Ops:
  0.0 18.9 %copy-start = (bf16[1,96,8192]{2,1,0:T(8,128)(2,1)S(1)}, bf16[1,96,8192]{2,1,0:T(8,128)(2,1)}, u32[]{:S(2)}) copy-start(bf16[1,96,8192]{2,1,0:T(8,128)(2,1)} %param.11) | copy-start | bytes 4718596
  3.7 39.3 %all-to-all-start = ((bf16[16,16,896]{2,1,0:T(8,128)(2,1)}), bf16[16,16,896]{2,1,0:T(8,128)(2,1)S(1)}, u32[]{:S(2)}, u32[]{:S(2)}) async-start(bf16[16,16,896]{2,1,0:T(8,128)(2,1)} %broadcast_in_dim.14), calls=%async_computation | async-start | bytes 917504 | tf_op jit(solution)/shard_map/all_to_all | solution.py:22
  24.4 16.4 %collective-permute-start = (bf16[96,2048]{1,0:T(8,128)(2,1)}, bf16[96,2048]{1,0:T(8,128)(2,1)S(1)}, u32[]{:S(2)}, u32[]{:S(2)}) collective-permute-start(bf16[96,2048]{1,0:T(8,128)(2,1)} %get-tuple-element.27), channel_id=1, source_target_pairs={{0,16},{16,32},{32,48},{48,0},{1,17},{17,33},{33,49},{49,1},{2,18}... | collective-permute-start | bytes 1179656 | tf_op jit(solution)/shard_map/ppermute | solution.py:130
  27.9 21.2 %collective-permute-start.1 = (bf16[96,2048]{1,0:T(8,128)(2,1)}, bf16[96,2048]{1,0:T(8,128)(2,1)}, u32[]{:S(2)}, u32[]{:S(2)}) collective-permute-start(bf16[96,2048]{1,0:T(8,128)(2,1)} %get-tuple-element.26), channel_id=1, source_target_pairs={{0,32},{16,48},{32,0},{48,16},{1,33},{17,49},{33,1},{49,17},{2,34}... | collective-permute-start | bytes 1179656 | tf_op jit(solution)/shard_map/ppermute | solution.py:130
  32.7 17.4 %collective-permute-start.2 = (bf16[96,2048]{1,0:T(8,128)(2,1)}, bf16[96,2048]{1,0:T(8,128)(2,1)S(1)}, u32[]{:S(2)}, u32[]{:S(2)}) collective-permute-start(bf16[96,2048]{1,0:T(8,128)(2,1)} %get-tuple-element.25), channel_id=1, source_target_pairs={{0,48},{16,0},{32,16},{48,32},{1,49},{17,1},{33,17},{49,33},{2,50}... | collective-permute-start | bytes 1179656 | tf_op jit(solution)/shard_map/ppermute | solution.py:130
  36.0 14.2 %collective-permute-start.3 = (bf16[6144,128]{1,0:T(8,128)(2,1)}, bf16[6144,128]{1,0:T(8,128)(2,1)}, u32[]{:S(2)}, u32[]{:S(2)}) collective-permute-start(bf16[6144,128]{1,0:T(8,128)(2,1)} %bitcast.44.g0), channel_id=1, source_target_pairs={{0,8},{8,0},{1,9},{9,1},{2,10},{10,2},{3,11},{11,3},{4,12},{12,4},... | collective-permute-start | bytes 4718600 | tf_op jit(solution)/shard_map/ppermute | solution.py:106
  37.9 12.3 %collective-permute-start.4 = (bf16[6144,128]{1,0:T(8,128)(2,1)}, bf16[6144,128]{1,0:T(8,128)(2,1)}, u32[]{:S(2)}, u32[]{:S(2)}) collective-permute-start(bf16[6144,128]{1,0:T(8,128)(2,1)} %bitcast.45.u0), channel_id=1, source_target_pairs={{0,8},{8,0},{1,9},{9,1},{2,10},{10,2},{3,11},{11,3},{4,12},{12,4},... | collective-permute-start | bytes 4718600 | tf_op jit(solution)/shard_map/ppermute | solution.py:107
  44.8 14.7 %all-to-all-start.1 = ((bf16[4,128,768]{2,1,0:T(8,128)(2,1)}), bf16[4,128,768]{2,1,0:T(8,128)(2,1)S(1)}, u32[]{:S(2)}, u32[]{:S(2)}) async-start(bf16[4,128,768]{2,1,0:T(8,128)(2,1)} %pad_maximum_fusion), calls=%async_computation.1 | async-start | bytes 1572864 | tf_op jit(solution)/shard_map/all_to_all | solution.py:161
  60.3 19.2 %collective-permute-start.5 = (bf16[64,6144]{1,0:T(8,128)(2,1)S(1)}, bf16[64,6144]{1,0:T(8,128)(2,1)S(1)}, u32[]{:S(2)}, u32[]{:S(2)}) collective-permute-start(bf16[64,6144]{1,0:T(8,128)(2,1)S(1)} %get-tuple-element.57), channel_id=1, source_target_pairs={{0,16},{16,32},{32,48},{48,0},{1,17},{17,33},{33,49},{49,1},{2,18}... | collective-permute-start | bytes 2359304 | tf_op jit(solution)/shard_map/ppermute | solution.py:170
  63.8 17.9 %collective-permute-start.6 = (bf16[64,6144]{1,0:T(8,128)(2,1)S(1)}, bf16[64,6144]{1,0:T(8,128)(2,1)S(1)}, u32[]{:S(2)}, u32[]{:S(2)}) collective-permute-start(bf16[64,6144]{1,0:T(8,128)(2,1)S(1)} %get-tuple-element.57), channel_id=1, source_target_pairs={{0,48},{16,0},{32,16},{48,32},{1,49},{17,1},{33,17},{49,33},{2,50}... | collective-permute-start | bytes 2359304 | tf_op jit(solution)/shard_map/ppermute | solution.py:171
  70.1 53.7 %collective-permute-start.9 = (bf16[384,2048]{1,0:T(8,128)(2,1)S(1)}, bf16[384,2048]{1,0:T(8,128)(2,1)}, u32[]{:S(2)}, u32[]{:S(2)}) collective-permute-start(bf16[384,2048]{1,0:T(8,128)(2,1)S(1)} %bitcast.163), channel_id=1, source_target_pairs={{0,8},{8,0},{1,9},{9,1},{2,10},{10,2},{3,11},{11,3},{4,12},{12,4},... | collective-permute-start | bytes 4718600 | tf_op jit(solution)/shard_map/ppermute | solution.py:169
  79.5 10.9 %collective-permute-start.7 = (bf16[32,6144]{1,0:T(8,128)(2,1)S(1)}, bf16[32,6144]{1,0:T(8,128)(2,1)S(1)}, u32[]{:S(2)}, u32[]{:S(2)}) collective-permute-start(bf16[32,6144]{1,0:T(8,128)(2,1)S(1)} %slice.153), channel_id=1, source_target_pairs={{0,16},{16,32},{32,48},{48,0},{1,17},{17,33},{33,49},{49,1},{2,18}... | collective-permute-start | bytes 1179656 | tf_op jit(solution)/shard_map/ppermute | solution.py:173
  81.8 10.1 %collective-permute-start.8 = (bf16[32,6144]{1,0:T(8,128)(2,1)S(1)}, bf16[32,6144]{1,0:T(8,128)(2,1)S(1)}, u32[]{:S(2)}, u32[]{:S(2)}) collective-permute-start(bf16[32,6144]{1,0:T(8,128)(2,1)S(1)} %slice.154), channel_id=1, source_target_pairs={{0,48},{16,0},{32,16},{48,32},{1,49},{17,1},{33,17},{49,33},{2,50}... | collective-permute-start | bytes 1179656 | tf_op jit(solution)/shard_map/ppermute | solution.py:174
  98.6 19.4 %collective-permute-start.13 = (bf16[256,256]{1,0:T(8,128)(2,1)}, bf16[256,256]{1,0:T(8,128)(2,1)S(1)}, u32[]{:S(2)}, u32[]{:S(2)}) collective-permute-start(bf16[256,256]{1,0:T(8,128)(2,1)} %gated.1), channel_id=1, source_target_pairs={{0,256},{64,320},{128,384},{192,448},{256,0},{320,64},{384,128},{4... | collective-permute-start | bytes 393224 | tf_op jit(solution)/shard_map/ppermute | solution.py:193
  107.2 20.5 %collective-permute-start.10 = (bf16[256,256]{1,0:T(8,128)(2,1)}, bf16[256,256]{1,0:T(8,128)(2,1)S(1)}, u32[]{:S(2)}, u32[]{:S(2)}) collective-permute-start(bf16[256,256]{1,0:T(8,128)(2,1)} %gated.1), channel_id=1, source_target_pairs={{0,64},{64,0},{128,192},{192,128},{256,320},{320,256},{384,448},{4... | collective-permute-start | bytes 393224 | tf_op jit(solution)/shard_map/ppermute | solution.py:194
  109.1 22.2 %collective-permute-start.11 = (bf16[256,256]{1,0:T(8,128)(2,1)}, bf16[256,256]{1,0:T(8,128)(2,1)S(1)}, u32[]{:S(2)}, u32[]{:S(2)}) collective-permute-start(bf16[256,256]{1,0:T(8,128)(2,1)} %gated.1), channel_id=1, source_target_pairs={{0,128},{64,192},{128,0},{192,64},{256,384},{320,448},{384,256},{4... | collective-permute-start | bytes 393224 | tf_op jit(solution)/shard_map/ppermute | solution.py:194
  115.6 17.3 %collective-permute-start.12 = (bf16[256,256]{1,0:T(8,128)(2,1)}, bf16[256,256]{1,0:T(8,128)(2,1)S(1)}, u32[]{:S(2)}, u32[]{:S(2)}) collective-permute-start(bf16[256,256]{1,0:T(8,128)(2,1)} %gated.1), channel_id=1, source_target_pairs={{0,192},{64,128},{128,64},{192,0},{256,448},{320,384},{384,320},{4... | collective-permute-start | bytes 393224 | tf_op jit(solution)/shard_map/ppermute | solution.py:194
  118.1 15.5 %collective-permute-start.15 = (bf16[256,256]{1,0:T(8,128)(2,1)S(1)}, bf16[256,256]{1,0:T(8,128)(2,1)S(1)}, u32[]{:S(2)}, u32[]{:S(2)}) collective-permute-start(bf16[256,256]{1,0:T(8,128)(2,1)S(1)} %collective-permute-done.13), channel_id=1, source_target_pairs={{0,128},{64,192},{128,0},{192,64},{256,384},{320,448},{384,256},{4... | collective-permute-start | bytes 393224 | tf_op jit(solution)/shard_map/ppermute | solution.py:195
  123.8 12.4 %collective-permute-start.16 = (bf16[256,256]{1,0:T(8,128)(2,1)S(1)}, bf16[256,256]{1,0:T(8,128)(2,1)S(1)}, u32[]{:S(2)}, u32[]{:S(2)}) collective-permute-start(bf16[256,256]{1,0:T(8,128)(2,1)S(1)} %collective-permute-done.13), channel_id=1, source_target_pairs={{0,192},{64,128},{128,64},{192,0},{256,448},{320,384},{384,320},{4... | collective-permute-start | bytes 393224 | tf_op jit(solution)/shard_map/ppermute | solution.py:195
  127.7 8.8 %collective-permute-start.14 = (bf16[256,256]{1,0:T(8,128)(2,1)S(1)}, bf16[256,256]{1,0:T(8,128)(2,1)S(1)}, u32[]{:S(2)}, u32[]{:S(2)}) collective-permute-start(bf16[256,256]{1,0:T(8,128)(2,1)S(1)} %collective-permute-done.13), channel_id=1, source_target_pairs={{0,64},{64,0},{128,192},{192,128},{256,320},{320,256},{384,448},{4... | collective-permute-start | bytes 393224 | tf_op jit(solution)/shard_map/ppermute | solution.py:195
  131.7 1.5 copy-start.1
  149.2 34.9 %copy-start.2 = (f32[16,2]{0,1:T(2,128)S(1)}, f32[16,2]{0,1:T(2,128)}, u32[]{:S(2)}) copy-start(f32[16,2]{0,1:T(2,128)} %param.8) | copy-start | bytes 388
  150.1 24.3 %all-to-all-start.3 = ((bf16[16,8,768]{2,1,0:T(8,128)(2,1)}), bf16[16,8,768]{2,1,0:T(8,128)(2,1)S(1)}, u32[]{:S(2)}, u32[]{:S(2)}) async-start(bf16[16,8,768]{2,1,0:T(8,128)(2,1)} %bitcast.69), calls=%async_computation.3 | async-start | bytes 393216 | tf_op jit(solution)/shard_map/all_to_all | solution.py:213
  175.0 9.1 %all-to-all-start.4 = ((bf16[4,16,768]{2,1,0:T(8,128)(2,1)}), bf16[4,16,768]{2,1,0:T(8,128)(2,1)S(1)}, u32[]{:S(2)}, u32[]{:S(2)}) async-start(bf16[4,16,768]{2,1,0:T(8,128)(2,1)} %pad_maximum_fusion.3), calls=%async_computation.4 | async-start | bytes 196608 | tf_op jit(solution)/shard_map/all_to_all | solution.py:217

commit v5 on v4

--- a/solution.py
+++ b/solution.py
@@ -1,3 +1,5 @@
+import functools
+
 import jax
 import jax.numpy as jnp
 from jax import lax
@@ -18,20 +20,62 @@
     return [(i, i ^ mask) for i in range(axis_size)]
 
 
-def everyone(value, axis, count):
-    return lax.all_to_all(
-        jnp.broadcast_to(value[None], (count,) + value.shape), axis, 0, 0, tiled=True
-    )
-
-
-def slot_numbers(expert_ids, capacity):
-    flat = expert_ids.reshape(-1)
-    pairs = flat.shape[0]
-    same = flat[:, None] == flat[None, :]
-    index = jnp.arange(pairs, dtype=jnp.int32)
-    earlier = index[None, :] < index[:, None]
-    position = jnp.sum((same & earlier).astype(jnp.int32), axis=1)
-    return (flat * capacity + position).reshape(expert_ids.shape)
+def numbered_kernel(ids_ref, tokens_ref, copies_ref, slot_ref, *, capacity):
+    block, width = tokens_ref.shape
+    row = lax.broadcasted_iota(jnp.int32, (block, block), 0)
+    column = lax.broadcasted_iota(jnp.int32, (block, block), 1)
+    named = [jnp.broadcast_to(ids_ref[k : k + 1, :], (block, block)) for k in range(2)]
+    lane = lax.broadcasted_iota(jnp.int32, (block, 128), 1)
+    tail = jnp.zeros((block, 128), jnp.int32)
+    for k in range(2):
+        mine = jnp.sum(jnp.where(row == column, named[k], 0), axis=1, keepdims=True)
+        same = (named[0] == mine).astype(jnp.int32) + (named[1] == mine).astype(jnp.int32)
+        earlier = jnp.sum(jnp.where(column < row, same, 0), axis=1, keepdims=True)
+        tail = jnp.where(lane == k, mine * capacity + earlier, tail)
+    slot_ref[...] = tail
+    whole = jnp.concatenate(
+        [tokens_ref[...], tail.astype(jnp.float32).astype(tokens_ref.dtype)], axis=1
+    )
+    copies_ref[...] = jnp.broadcast_to(whole[None], copies_ref.shape)
+
+
+def numbered(expert_ids, tokens, capacity, copies):
+    block, width = tokens.shape
+    return pl.pallas_call(
+        functools.partial(numbered_kernel, capacity=capacity),
+        out_shape=(
+            jax.ShapeDtypeStruct((copies, block, width + 128), tokens.dtype),
+            jax.ShapeDtypeStruct((block, 128), jnp.int32),
+        ),
+        name="numbered",
+    )(expert_ids.T, tokens)
+
+
+def dealt_kernel(at_ref, w_ref, *out_refs, span):
+    count = len(out_refs)
+    for k, out_ref in enumerate(out_refs):
+        to = lax.rem(at_ref[0] + k, count)
+        for j in range(out_ref.shape[1] // span):
+            z = at_ref[1] ^ j
+            at = pl.multiple_of((z * count + to) * span, span)
+            out_ref[:, j * span : (j + 1) * span] = w_ref[0, :, pl.ds(at, span)]
+
+
+def dealt(y_here, z_here, w, count, span):
+    _, rows, units = w.shape
+    return pl.pallas_call(
+        functools.partial(dealt_kernel, span=span),
+        out_shape=[jax.ShapeDtypeStruct((rows, units // count), w.dtype)] * count,
+        in_specs=[
+            pl.BlockSpec(memory_space=pltpu.SMEM),
+            pl.BlockSpec(memory_space=pltpu.VMEM),
+        ],
+        out_specs=[pl.BlockSpec(memory_space=pltpu.VMEM)] * count,
+        cost_estimate=pl.CostEstimate(
+            flops=4_000_000, transcendentals=0, bytes_accessed=rows * units * 4
+        ),
+        name="dealt",
+    )(jnp.stack([y_here, z_here]).astype(jnp.int32), w)
 
 
 DEPTH = 2048
@@ -107,32 +151,19 @@
     up_far = lax.ppermute(up_own, "c", SWAP)
     features = w_down_t.shape[1]
     z_here = lax.axis_index("zl")
-    order = range(zl)
     span = c * units
     y_here = lax.axis_index("y")
 
-    def columns(shift):
-        at = ((y_here + shift) % y) * span
-        return jnp.concatenate(
-            [
-                lax.dynamic_slice_in_dim(
-                    w_down_t[0], (z_here ^ j) * (y * span) + at, span, 1
-                )
-                for j in order
-            ],
-            axis=1,
-        )
-
+    columns = dealt(y_here, z_here, w_down_t, y, span)
     down = jnp.zeros((y, features, zl * span), bf16)
     for k in range(y):
-        moved = columns(k)
+        moved = columns[k]
         if k:
             moved = lax.ppermute(moved, "y", step(y, k))
         down = lax.dynamic_update_slice_in_dim(down, moved[None], (y_here - k) % y, 0)
     down = down.reshape(y * features, zl * span)
-    slot = slot_numbers(expert_ids, capacity)
-    tail = jnp.pad(slot, ((0, 0), (0, 126)), constant_values=0).astype(bf16)
-    seen = everyone(jnp.concatenate([tokens, tail], axis=1), ("zh", "zl"), zh * zl)
+    copies, slot = numbered(expert_ids, tokens, capacity, zh * zl)
+    seen = lax.all_to_all(copies, ("zh", "zl"), 0, 0, tiled=True)
     seen = seen.reshape(zh, zl * block, width + 128)
     slot_seen = seen[0, :, width : width + 2].astype(f32).astype(jnp.int32)
 
@@ -194,9 +225,11 @@
     near = [lax.ppermute(hidden, "zl", flip(zl, k)) for k in (1, 2, 3)]
     distant = [lax.ppermute(other, "zl", flip(zl, k)) for k in (1, 2, 3)]
     pairs = [hidden, *near, other, *distant]
-    both = jnp.concatenate(
-        [jnp.where(first, down, down_far), jnp.where(first, down_far, down)], axis=0
-    )
+    own = down.reshape(y, features, zl * span)
+    far = down_far.reshape(y, features, zl * span)
+    both = jnp.stack(
+        [jnp.where(first, own, far), jnp.where(first, far, own)], axis=1
+    ).reshape(width, zl * span)
     part = out(pairs, both)
     parts = [part[n * rows : (n + 1) * rows] for n in range(y)]
 
@@ -229,8 +262,7 @@
         pick = (slot[:, k][:, None] == every[None, :]).astype(bf16)
         picked = jnp.dot(pick, result, preferred_element_type=f32)
         mixed = mixed + gate_probs[:, k][:, None] * picked
-    mixed = mixed.astype(bf16).reshape(block, c, y, features)
-    return mixed.transpose(0, 2, 1, 3).reshape(block, width)
+    return mixed.astype(bf16)
 
 
 def solution(mesh):

time: 186 us -> 181 us (0.973)
  local copies, waits for them, and re-layouts: 19.8 us -> 13 us
  waiting for transfers between devices: 42.3 us -> 44.5 us
    unnamed x40 -> x32, local copies, waits for them, and re-layouts: 14 us -> 8.3 us
    all_to_all x1, waiting for transfers between devices: 2.09 us -> 5.1 us  [per_device(): seen = lax.all_to_all(copies, ('zh', 'zl'), 0, 0, tiled=True)]
    pallas_call x0 -> x1, local copies, waits for them, and re-layouts: none -> 2.53 us  [dealt(): pl.pallas_call(functools.partial(dealt_kernel, span=span), out_shape=[jax...]
  transfers between devices with their start and end apart: 21 -> 21, of which waited for: 9 -> 9; matrix products, arithmetic and copies ran while one was open for 11% -> 9% of each run, Pallas kernels for 3% -> 3%
where the time goes in v5:
time: 181 us; the launch traced here: 180 us
  starting transfers between devices  94.3 us (52%)
  waiting for transfers between devices  44.5 us (25%)
  local copies, waits for them, and re-layouts  13 us (7%)
  blocking collectives  12 us (7%)
  Pallas kernels  7.65 us (4%)
  matrix products  4.09 us (2%)
  other arithmetic  3.8 us (2%)
    all_to_all x1, starting transfers between devices, per_device(): seen = lax.all_to_all(copies, ('zh', 'zl'), 0, 0, tiled=True)  15.2 us
    all_to_all x1, waiting for transfers between devices, per_device(): result = lax.all_to_all(result, ('zh', 'zl'), 0, 0, tiled=True)  13.5 us
    all_to_all x1, blocking collectives, per_device(): part = lax.all_to_all(part, 'y', 0, 0, tiled=True).astype(f32)  12 us
    ppermute x3, starting transfers between devices, per_device(): moved = lax.ppermute(moved, 'y', step(y, k))  11.5 us
    ppermute x3, starting transfers between devices, per_device(): near = [lax.ppermute(hidden, 'zl', flip(zl, k)) for k in (1, 2, 3)]  11.4 us
    all_to_all x1, waiting for transfers between devices, per_device(): arrived = lax.all_to_all(slots, 'x', 0, 0, tiled=True)  10.3 us
    ppermute x3, starting transfers between devices, per_device(): distant = [lax.ppermute(other, 'zl', flip(zl, k)) for k in (1, 2, 3)]  10.1 us
    all_to_all x1, starting transfers between devices, per_device(): result = lax.all_to_all(result, ('zh', 'zl'), 0, 0, tiled=True)  9.58 us
  transfers between devices with their start and end apart: 21, of which 9 were waited for; matrix products, arithmetic and copies ran while one was open for 9% of the time, Pallas kernels for 3%

profile of v5, /device:TPU:32, one launch (start us, length us, event | category | flops | bytes accessed | tf_op | source)
XLA Modules:
  0.0 180.1 jit_solution(1862001531941100216)
XLA Ops:
  1.7 15.2 %all-to-all-start = ((bf16[16,16,896]{2,1,0:T(8,128)(2,1)}), bf16[16,16,896]{2,1,0:T(8,128)(2,1)S(1)}, u32[]{:S(2)}, u32[]{:S(2)}) async-start(bf16[16,16,896]{2,1,0:T(8,128)(2,1)} %get-tuple-element.18), calls=%async_computation | async-start | bytes 917504 | tf_op jit(solution)/shard_map/all_to_all | solution.py:166
  17.2 2.5 %dealt.1 = (bf16[4,96,2048]{2,1,0:T(8,128)(2,1)S(1)}, bf16[96,2048]{1,0:T(8,128)(2,1)}, bf16[96,2048]{1,0:T(8,128)(2,1)}, bf16[96,2048]{1,0:T(8,128)(2,1)}) fusion(bf16[4,96,2048]{2,1,0:T(8,128)(2,1)S(1)} %broadcast_in_dim.12, s32[]{:T(128)S(6)} %select_n.147, s32[2]{0:T(128)S(1)} %pad_add_fusion, bf16[1,96,8192]{2,1,0:T(8,128)(2,1)} %param.11), kind=kCustom, calls=%fused_computation.35 | custom fusion | bytes 3146244 | tf_op jit(solution)/shard_map/dealt/pallas_call | solution.py:66
  19.7 3.5 %collective-permute-start = (bf16[96,2048]{1,0:T(8,128)(2,1)}, bf16[96,2048]{1,0:T(8,128)(2,1)S(1)}, u32[]{:S(2)}, u32[]{:S(2)}) collective-permute-start(bf16[96,2048]{1,0:T(8,128)(2,1)} %get-tuple-element.34), channel_id=1, source_target_pairs={{0,16},{16,32},{32,48},{48,0},{1,17},{17,33},{33,49},{49,1},{2,18}... | collective-permute-start | bytes 1179656 | tf_op jit(solution)/shard_map/ppermute | solution.py:162
  23.2 4.8 %collective-permute-start.1 = (bf16[96,2048]{1,0:T(8,128)(2,1)}, bf16[96,2048]{1,0:T(8,128)(2,1)S(1)}, u32[]{:S(2)}, u32[]{:S(2)}) collective-permute-start(bf16[96,2048]{1,0:T(8,128)(2,1)} %get-tuple-element.36), channel_id=1, source_target_pairs={{0,32},{16,48},{32,0},{48,16},{1,33},{17,49},{33,1},{49,17},{2,34}... | collective-permute-start | bytes 1179656 | tf_op jit(solution)/shard_map/ppermute | solution.py:162
  28.0 3.3 %collective-permute-start.2 = (bf16[96,2048]{1,0:T(8,128)(2,1)}, bf16[96,2048]{1,0:T(8,128)(2,1)S(1)}, u32[]{:S(2)}, u32[]{:S(2)}) collective-permute-start(bf16[96,2048]{1,0:T(8,128)(2,1)} %get-tuple-element.38), channel_id=1, source_target_pairs={{0,48},{16,0},{32,16},{48,32},{1,49},{17,1},{33,17},{49,33},{2,50}... | collective-permute-start | bytes 1179656 | tf_op jit(solution)/shard_map/ppermute | solution.py:162
  36.0 5.1 %all-to-all-done = bf16[16,16,896]{2,1,0:T(8,128)(2,1)S(1)} async-done(((bf16[16,16,896]{2,1,0:T(8,128)(2,1)}), bf16[16,16,896]{2,1,0:T(8,128)(2,1)S(1)}, u32[]{:S(2)}, u32[]{:S(2)}) %all-to-all-start) | async-done | bytes 458784 | tf_op jit(solution)/shard_map/all_to_all | solution.py:166
  42.8 4.3 %all-to-all-start.1 = ((bf16[4,128,768]{2,1,0:T(8,128)(2,1)}), bf16[4,128,768]{2,1,0:T(8,128)(2,1)S(1)}, u32[]{:S(2)}, u32[]{:S(2)}) async-start(bf16[4,128,768]{2,1,0:T(8,128)(2,1)} %pad_maximum_fusion.1), calls=%async_computation.1 | async-start | bytes 1572864 | tf_op jit(solution)/shard_map/all_to_all | solution.py:192
  47.2 10.3 %all-to-all-done.1 = bf16[4,128,768]{2,1,0:T(8,128)(2,1)S(1)} async-done(((bf16[4,128,768]{2,1,0:T(8,128)(2,1)}), bf16[4,128,768]{2,1,0:T(8,128)(2,1)S(1)}, u32[]{:S(2)}, u32[]{:S(2)}) %all-to-all-start.1) | async-done | bytes 786464 | tf_op jit(solution)/shard_map/all_to_all | solution.py:192
  58.3 3.5 %collective-permute-start.5 = (bf16[64,6144]{1,0:T(8,128)(2,1)S(1)}, bf16[64,6144]{1,0:T(8,128)(2,1)S(1)}, u32[]{:S(2)}, u32[]{:S(2)}) collective-permute-start(bf16[64,6144]{1,0:T(8,128)(2,1)S(1)} %get-tuple-element.43), channel_id=1, source_target_pairs={{0,16},{16,32},{32,48},{48,0},{1,17},{17,33},{33,49},{49,1},{2,18}... | collective-permute-start | bytes 2359304 | tf_op jit(solution)/shard_map/ppermute | solution.py:201
  61.8 3.6 %collective-permute-start.6 = (bf16[64,6144]{1,0:T(8,128)(2,1)S(1)}, bf16[64,6144]{1,0:T(8,128)(2,1)S(1)}, u32[]{:S(2)}, u32[]{:S(2)}) collective-permute-start(bf16[64,6144]{1,0:T(8,128)(2,1)S(1)} %get-tuple-element.43), channel_id=1, source_target_pairs={{0,48},{16,0},{32,16},{48,32},{1,49},{17,1},{33,17},{49,33},{2,50}... | collective-permute-start | bytes 2359304 | tf_op jit(solution)/shard_map/ppermute | solution.py:202
  71.9 5.5 %collective-permute-done.5 = bf16[64,6144]{1,0:T(8,128)(2,1)S(1)} collective-permute-done((bf16[64,6144]{1,0:T(8,128)(2,1)S(1)}, bf16[64,6144]{1,0:T(8,128)(2,1)S(1)}, u32[]{:S(2)}, u32[]{:S(2)}) %collective-permute-start.5) | collective-permute-done | bytes 786464 | tf_op jit(solution)/shard_map/ppermute | solution.py:201
  79.7 4.8 %collective-permute-start.8 = (bf16[32,6144]{1,0:T(8,128)(2,1)S(1)}, bf16[32,6144]{1,0:T(8,128)(2,1)S(1)}, u32[]{:S(2)}, u32[]{:S(2)}) collective-permute-start(bf16[32,6144]{1,0:T(8,128)(2,1)S(1)} %slice.152), channel_id=1, source_target_pairs={{0,48},{16,0},{32,16},{48,32},{1,49},{17,1},{33,17},{49,33},{2,50}... | collective-permute-start | bytes 1179656 | tf_op jit(solution)/shard_map/ppermute | solution.py:205
  90.6 5.9 %gated.1 = bf16[256,256]{1,0:T(8,128)(2,1)} custom-call(s32[1]{0:T(128)} %bitcast.core_ref, bf16[256,6144]{1,0:T(8,128)(2,1)} %constant_dynamic-update-slice_fusion.rows_ref, bf16[6144,128]{1,0:T(8,128)(2,1)} %bitcast.119, bf16[6144,128]{1,0:T(8,128)(2,1)} %bitcast.121, bf16[6144,128]{1,0:T(8,128)(2,1)} %collective-permute-done.3.g1, ...), custom_call_target="tpu_custom_call" | custom-call | flops 1610612736 | bytes 9437184 | tf_op jit(solution)/shard_map/gated/pallas_call | solution.py:117
  96.6 8.5 %collective-permute-start.13 = (bf16[256,256]{1,0:T(8,128)(2,1)}, bf16[256,256]{1,0:T(8,128)(2,1)S(1)}, u32[]{:S(2)}, u32[]{:S(2)}) collective-permute-start(bf16[256,256]{1,0:T(8,128)(2,1)} %gated.1), channel_id=1, source_target_pairs={{0,256},{64,320},{128,384},{192,448},{256,0},{320,64},{384,128},{4... | collective-permute-start | bytes 393224 | tf_op jit(solution)/shard_map/ppermute | solution.py:224
  107.0 6.1 %collective-permute-start.11 = (bf16[256,256]{1,0:T(8,128)(2,1)}, bf16[256,256]{1,0:T(8,128)(2,1)S(1)}, u32[]{:S(2)}, u32[]{:S(2)}) collective-permute-start(bf16[256,256]{1,0:T(8,128)(2,1)} %gated.1), channel_id=1, source_target_pairs={{0,128},{64,192},{128,0},{192,64},{256,384},{320,448},{384,256},{4... | collective-permute-start | bytes 393224 | tf_op jit(solution)/shard_map/ppermute | solution.py:225
  113.2 3.4 %collective-permute-start.10 = (bf16[256,256]{1,0:T(8,128)(2,1)}, bf16[256,256]{1,0:T(8,128)(2,1)S(1)}, u32[]{:S(2)}, u32[]{:S(2)}) collective-permute-start(bf16[256,256]{1,0:T(8,128)(2,1)} %gated.1), channel_id=1, source_target_pairs={{0,64},{64,0},{128,192},{192,128},{256,320},{320,256},{384,448},{4... | collective-permute-start | bytes 393224 | tf_op jit(solution)/shard_map/ppermute | solution.py:225
  116.6 3.4 %collective-permute-start.16 = (bf16[256,256]{1,0:T(8,128)(2,1)S(1)}, bf16[256,256]{1,0:T(8,128)(2,1)S(1)}, u32[]{:S(2)}, u32[]{:S(2)}) collective-permute-start(bf16[256,256]{1,0:T(8,128)(2,1)S(1)} %collective-permute-done.13), channel_id=1, source_target_pairs={{0,192},{64,128},{128,64},{192,0},{256,448},{320,384},{384,320},{4... | collective-permute-start | bytes 393224 | tf_op jit(solution)/shard_map/ppermute | solution.py:226
  120.0 3.4 %collective-permute-start.15 = (bf16[256,256]{1,0:T(8,128)(2,1)S(1)}, bf16[256,256]{1,0:T(8,128)(2,1)S(1)}, u32[]{:S(2)}, u32[]{:S(2)}) collective-permute-start(bf16[256,256]{1,0:T(8,128)(2,1)S(1)} %collective-permute-done.13), channel_id=1, source_target_pairs={{0,128},{64,192},{128,0},{192,64},{256,384},{320,448},{384,256},{4... | collective-permute-start | bytes 393224 | tf_op jit(solution)/shard_map/ppermute | solution.py:226
  125.6 3.4 %collective-permute-start.14 = (bf16[256,256]{1,0:T(8,128)(2,1)S(1)}, bf16[256,256]{1,0:T(8,128)(2,1)S(1)}, u32[]{:S(2)}, u32[]{:S(2)}) collective-permute-start(bf16[256,256]{1,0:T(8,128)(2,1)S(1)} %collective-permute-done.13), channel_id=1, source_target_pairs={{0,64},{64,0},{128,192},{192,128},{256,320},{320,256},{384,448},{4... | collective-permute-start | bytes 393224 | tf_op jit(solution)/shard_map/ppermute | solution.py:226
  133.1 12.0 %all_to_all.25 = bf16[4,64,768]{2,1,0:T(8,128)(2,1)S(1)} all-to-all(bf16[4,64,768]{2,1,0:T(8,128)(2,1)S(1)} %constant_dynamic-slice_fusion), channel_id=1, replica_groups=mesh['zl'=8,'y'=4,'c'=2,'zh'=2,'x'=4] {'y'}, dimensions={0} | all-to-all | bytes 786432 | tf_op jit(solution)/shard_map/all_to_all | solution.py:240
  146.0 9.6 %all-to-all-start.3 = ((bf16[16,8,768]{2,1,0:T(8,128)(2,1)}), bf16[16,8,768]{2,1,0:T(8,128)(2,1)S(1)}, u32[]{:S(2)}, u32[]{:S(2)}) async-start(bf16[16,8,768]{2,1,0:T(8,128)(2,1)} %bitcast.42), calls=%async_computation.3 | async-start | bytes 393216 | tf_op jit(solution)/shard_map/all_to_all | solution.py:246
  155.6 13.5 %all-to-all-done.3 = bf16[16,8,768]{2,1,0:T(8,128)(2,1)S(1)} async-done(((bf16[16,8,768]{2,1,0:T(8,128)(2,1)}), bf16[16,8,768]{2,1,0:T(8,128)(2,1)S(1)}, u32[]{:S(2)}, u32[]{:S(2)}) %all-to-all-start.3) | async-done | bytes 196640 | tf_op jit(solution)/shard_map/all_to_all | solution.py:246
  169.8 3.3 %all-to-all-start.4 = ((bf16[4,16,768]{2,1,0:T(8,128)(2,1)}), bf16[4,16,768]{2,1,0:T(8,128)(2,1)S(1)}, u32[]{:S(2)}, u32[]{:S(2)}) async-start(bf16[4,16,768]{2,1,0:T(8,128)(2,1)} %pad_maximum_fusion.2), calls=%async_computation.4 | async-start | bytes 196608 | tf_op jit(solution)/shard_map/all_to_all | solution.py:250
  173.1 5.8 %all-to-all-done.4 = bf16[4,16,768]{2,1,0:T(8,128)(2,1)S(1)} async-done(((bf16[4,16,768]{2,1,0:T(8,128)(2,1)}), bf16[4,16,768]{2,1,0:T(8,128)(2,1)S(1)}, u32[]{:S(2)}, u32[]{:S(2)}) %all-to-all-start.4) | async-done | bytes 98336 | tf_op jit(solution)/shard_map/all_to_all | solution.py:250
  (97 shorter events, 34.7 us)
Async XLA Ops:
  1.7 39.3 %all-to-all-start = ((bf16[16,16,896]{2,1,0:T(8,128)(2,1)}), bf16[16,16,896]{2,1,0:T(8,128)(2,1)S(1)}, u32[]{:S(2)}, u32[]{:S(2)}) async-start(bf16[16,16,896]{2,1,0:T(8,128)(2,1)} %get-tuple-element.18), calls=%async_computation | async-start | bytes 917504 | tf_op jit(solution)/shard_map/all_to_all | solution.py:166
  19.7 16.2 %collective-permute-start = (bf16[96,2048]{1,0:T(8,128)(2,1)}, bf16[96,2048]{1,0:T(8,128)(2,1)S(1)}, u32[]{:S(2)}, u32[]{:S(2)}) collective-permute-start(bf16[96,2048]{1,0:T(8,128)(2,1)} %get-tuple-element.34), channel_id=1, source_target_pairs={{0,16},{16,32},{32,48},{48,0},{1,17},{17,33},{33,49},{49,1},{2,18}... | collective-permute-start | bytes 1179656 | tf_op jit(solution)/shard_map/ppermute | solution.py:162
  23.2 23.9 %collective-permute-start.1 = (bf16[96,2048]{1,0:T(8,128)(2,1)}, bf16[96,2048]{1,0:T(8,128)(2,1)S(1)}, u32[]{:S(2)}, u32[]{:S(2)}) collective-permute-start(bf16[96,2048]{1,0:T(8,128)(2,1)} %get-tuple-element.36), channel_id=1, source_target_pairs={{0,32},{16,48},{32,0},{48,16},{1,33},{17,49},{33,1},{49,17},{2,34}... | collective-permute-start | bytes 1179656 | tf_op jit(solution)/shard_map/ppermute | solution.py:162
  28.0 19.1 %collective-permute-start.2 = (bf16[96,2048]{1,0:T(8,128)(2,1)}, bf16[96,2048]{1,0:T(8,128)(2,1)S(1)}, u32[]{:S(2)}, u32[]{:S(2)}) collective-permute-start(bf16[96,2048]{1,0:T(8,128)(2,1)} %get-tuple-element.38), channel_id=1, source_target_pairs={{0,48},{16,0},{32,16},{48,32},{1,49},{17,1},{33,17},{49,33},{2,50}... | collective-permute-start | bytes 1179656 | tf_op jit(solution)/shard_map/ppermute | solution.py:162
  31.3 15.9 %collective-permute-start.3 = (bf16[6144,128]{1,0:T(8,128)(2,1)}, bf16[6144,128]{1,0:T(8,128)(2,1)}, u32[]{:S(2)}, u32[]{:S(2)}) collective-permute-start(bf16[6144,128]{1,0:T(8,128)(2,1)} %bitcast.118), channel_id=1, source_target_pairs={{0,8},{8,0},{1,9},{9,1},{2,10},{10,2},{3,11},{11,3},{4,12},{12,4},... | collective-permute-start | bytes 4718600 | tf_op jit(solution)/shard_map/ppermute | solution.py:150
  33.2 14.0 %collective-permute-start.4 = (bf16[6144,128]{1,0:T(8,128)(2,1)}, bf16[6144,128]{1,0:T(8,128)(2,1)}, u32[]{:S(2)}, u32[]{:S(2)}) collective-permute-start(bf16[6144,128]{1,0:T(8,128)(2,1)} %bitcast.120), channel_id=1, source_target_pairs={{0,8},{8,0},{1,9},{9,1},{2,10},{10,2},{3,11},{11,3},{4,12},{12,4},... | collective-permute-start | bytes 4718600 | tf_op jit(solution)/shard_map/ppermute | solution.py:151
  42.8 14.7 %all-to-all-start.1 = ((bf16[4,128,768]{2,1,0:T(8,128)(2,1)}), bf16[4,128,768]{2,1,0:T(8,128)(2,1)S(1)}, u32[]{:S(2)}, u32[]{:S(2)}) async-start(bf16[4,128,768]{2,1,0:T(8,128)(2,1)} %pad_maximum_fusion.1), calls=%async_computation.1 | async-start | bytes 1572864 | tf_op jit(solution)/shard_map/all_to_all | solution.py:192
  58.3 19.2 %collective-permute-start.5 = (bf16[64,6144]{1,0:T(8,128)(2,1)S(1)}, bf16[64,6144]{1,0:T(8,128)(2,1)S(1)}, u32[]{:S(2)}, u32[]{:S(2)}) collective-permute-start(bf16[64,6144]{1,0:T(8,128)(2,1)S(1)} %get-tuple-element.43), channel_id=1, source_target_pairs={{0,16},{16,32},{32,48},{48,0},{1,17},{17,33},{33,49},{49,1},{2,18}... | collective-permute-start | bytes 2359304 | tf_op jit(solution)/shard_map/ppermute | solution.py:201
  61.8 17.9 %collective-permute-start.6 = (bf16[64,6144]{1,0:T(8,128)(2,1)S(1)}, bf16[64,6144]{1,0:T(8,128)(2,1)S(1)}, u32[]{:S(2)}, u32[]{:S(2)}) collective-permute-start(bf16[64,6144]{1,0:T(8,128)(2,1)S(1)} %get-tuple-element.43), channel_id=1, source_target_pairs={{0,48},{16,0},{32,16},{48,32},{1,49},{17,1},{33,17},{49,33},{2,50}... | collective-permute-start | bytes 2359304 | tf_op jit(solution)/shard_map/ppermute | solution.py:202
  68.0 52.0 %collective-permute-start.9 = (bf16[384,2048]{1,0:T(8,128)(2,1)S(1)}, bf16[384,2048]{1,0:T(8,128)(2,1)}, u32[]{:S(2)}, u32[]{:S(2)}) collective-permute-start(bf16[384,2048]{1,0:T(8,128)(2,1)S(1)} %bitcast.111), channel_id=1, source_target_pairs={{0,8},{8,0},{1,9},{9,1},{2,10},{10,2},{3,11},{11,3},{4,12},{12,4},... | collective-permute-start | bytes 4718600 | tf_op jit(solution)/shard_map/ppermute | solution.py:200
  77.5 10.9 %collective-permute-start.7 = (bf16[32,6144]{1,0:T(8,128)(2,1)S(1)}, bf16[32,6144]{1,0:T(8,128)(2,1)S(1)}, u32[]{:S(2)}, u32[]{:S(2)}) collective-permute-start(bf16[32,6144]{1,0:T(8,128)(2,1)S(1)} %slice.151), channel_id=1, source_target_pairs={{0,16},{16,32},{32,48},{48,0},{1,17},{17,33},{33,49},{49,1},{2,18}... | collective-permute-start | bytes 1179656 | tf_op jit(solution)/shard_map/ppermute | solution.py:204
  79.7 10.1 %collective-permute-start.8 = (bf16[32,6144]{1,0:T(8,128)(2,1)S(1)}, bf16[32,6144]{1,0:T(8,128)(2,1)S(1)}, u32[]{:S(2)}, u32[]{:S(2)}) collective-permute-start(bf16[32,6144]{1,0:T(8,128)(2,1)S(1)} %slice.152), channel_id=1, source_target_pairs={{0,48},{16,0},{32,16},{48,32},{1,49},{17,1},{33,17},{49,33},{2,50}... | collective-permute-start | bytes 1179656 | tf_op jit(solution)/shard_map/ppermute | solution.py:205
  96.6 20.0 %collective-permute-start.13 = (bf16[256,256]{1,0:T(8,128)(2,1)}, bf16[256,256]{1,0:T(8,128)(2,1)S(1)}, u32[]{:S(2)}, u32[]{:S(2)}) collective-permute-start(bf16[256,256]{1,0:T(8,128)(2,1)} %gated.1), channel_id=1, source_target_pairs={{0,256},{64,320},{128,384},{192,448},{256,0},{320,64},{384,128},{4... | collective-permute-start | bytes 393224 | tf_op jit(solution)/shard_map/ppermute | solution.py:224
  105.1 20.5 %collective-permute-start.12 = (bf16[256,256]{1,0:T(8,128)(2,1)}, bf16[256,256]{1,0:T(8,128)(2,1)S(1)}, u32[]{:S(2)}, u32[]{:S(2)}) collective-permute-start(bf16[256,256]{1,0:T(8,128)(2,1)} %gated.1), channel_id=1, source_target_pairs={{0,192},{64,128},{128,64},{192,0},{256,448},{320,384},{384,320},{4... | collective-permute-start | bytes 393224 | tf_op jit(solution)/shard_map/ppermute | solution.py:225
  107.0 22.2 %collective-permute-start.11 = (bf16[256,256]{1,0:T(8,128)(2,1)}, bf16[256,256]{1,0:T(8,128)(2,1)S(1)}, u32[]{:S(2)}, u32[]{:S(2)}) collective-permute-start(bf16[256,256]{1,0:T(8,128)(2,1)} %gated.1), channel_id=1, source_target_pairs={{0,128},{64,192},{128,0},{192,64},{256,384},{320,448},{384,256},{4... | collective-permute-start | bytes 393224 | tf_op jit(solution)/shard_map/ppermute | solution.py:225
  113.2 16.4 %collective-permute-start.10 = (bf16[256,256]{1,0:T(8,128)(2,1)}, bf16[256,256]{1,0:T(8,128)(2,1)S(1)}, u32[]{:S(2)}, u32[]{:S(2)}) collective-permute-start(bf16[256,256]{1,0:T(8,128)(2,1)} %gated.1), channel_id=1, source_target_pairs={{0,64},{64,0},{128,192},{192,128},{256,320},{320,256},{384,448},{4... | collective-permute-start | bytes 393224 | tf_op jit(solution)/shard_map/ppermute | solution.py:225
  116.6 14.1 %collective-permute-start.16 = (bf16[256,256]{1,0:T(8,128)(2,1)S(1)}, bf16[256,256]{1,0:T(8,128)(2,1)S(1)}, u32[]{:S(2)}, u32[]{:S(2)}) collective-permute-start(bf16[256,256]{1,0:T(8,128)(2,1)S(1)} %collective-permute-done.13), channel_id=1, source_target_pairs={{0,192},{64,128},{128,64},{192,0},{256,448},{320,384},{384,320},{4... | collective-permute-start | bytes 393224 | tf_op jit(solution)/shard_map/ppermute | solution.py:226
  120.0 11.1 %collective-permute-start.15 = (bf16[256,256]{1,0:T(8,128)(2,1)S(1)}, bf16[256,256]{1,0:T(8,128)(2,1)S(1)}, u32[]{:S(2)}, u32[]{:S(2)}) collective-permute-start(bf16[256,256]{1,0:T(8,128)(2,1)S(1)} %collective-permute-done.13), channel_id=1, source_target_pairs={{0,128},{64,192},{128,0},{192,64},{256,384},{320,448},{384,256},{4... | collective-permute-start | bytes 393224 | tf_op jit(solution)/shard_map/ppermute | solution.py:226
  125.3 4.6 %copy-start = (bf16[256,256]{1,0:T(8,128)(2,1)S(1)}, bf16[256,256]{1,0:T(8,128)(2,1)}, u32[]{:S(2)}) copy-start(bf16[256,256]{1,0:T(8,128)(2,1)} %gated.1) | copy-start | bytes 393220
  125.6 7.0 %collective-permute-start.14 = (bf16[256,256]{1,0:T(8,128)(2,1)S(1)}, bf16[256,256]{1,0:T(8,128)(2,1)S(1)}, u32[]{:S(2)}, u32[]{:S(2)}) collective-permute-start(bf16[256,256]{1,0:T(8,128)(2,1)S(1)} %collective-permute-done.13), channel_id=1, source_target_pairs={{0,64},{64,0},{128,192},{192,128},{256,320},{320,256},{384,448},{4... | collective-permute-start | bytes 393224 | tf_op jit(solution)/shard_map/ppermute | solution.py:226
  133.0 45.9 %copy-start.2 = (f32[16,2]{0,1:T(2,128)S(1)}, f32[16,2]{0,1:T(2,128)}, u32[]{:S(2)}) copy-start(f32[16,2]{0,1:T(2,128)} %param.8) | copy-start | bytes 388
  133.0 45.9 %copy-start.1 = (s32[16,128]{1,0:T(8,128)S(1)}, s32[16,128]{1,0:T(8,128)}, u32[]{:S(2)}) copy-start(s32[16,128]{1,0:T(8,128)} %get-tuple-element.29) | copy-start | bytes 24580
  146.0 23.1 %all-to-all-start.3 = ((bf16[16,8,768]{2,1,0:T(8,128)(2,1)}), bf16[16,8,768]{2,1,0:T(8,128)(2,1)S(1)}, u32[]{:S(2)}, u32[]{:S(2)}) async-start(bf16[16,8,768]{2,1,0:T(8,128)(2,1)} %bitcast.42), calls=%async_computation.3 | async-start | bytes 393216 | tf_op jit(solution)/shard_map/all_to_all | solution.py:246
  169.8 9.1 %all-to-all-start.4 = ((bf16[4,16,768]{2,1,0:T(8,128)(2,1)}), bf16[4,16,768]{2,1,0:T(8,128)(2,1)S(1)}, u32[]{:S(2)}, u32[]{:S(2)}) async-start(bf16[4,16,768]{2,1,0:T(8,128)(2,1)} %pad_maximum_fusion.2), calls=%async_computation.4 | async-start | bytes 196608 | tf_op jit(solution)/shard_map/all_to_all | solution.py:250

commit v6 on v5

--- a/solution.py
+++ b/solution.py
@@ -78,7 +78,7 @@
     )(jnp.stack([y_here, z_here]).astype(jnp.int32), w)
 
 
-DEPTH = 2048
+DEPTH = 3072
 
 
 def gated_kernel(core_ref, rows_ref, g0, u0, g1, u1, out_ref, gate, up):

time: 181 us -> 181 us (level)
  no operation moved by 1% of the time
where the time goes in v6:
time: 181 us; the launch traced here: 180 us
  starting transfers between devices  94.3 us (52%)
  waiting for transfers between devices  44.5 us (25%)
  local copies, waits for them, and re-layouts  13 us (7%)
  blocking collectives  12 us (7%)
  Pallas kernels  7.14 us (4%)
  matrix products  4.08 us (2%)
  other arithmetic  3.8 us (2%)
    all_to_all x1, starting transfers between devices, per_device(): seen = lax.all_to_all(copies, ('zh', 'zl'), 0, 0, tiled=True)  15.2 us
    all_to_all x1, waiting for transfers between devices, per_device(): result = lax.all_to_all(result, ('zh', 'zl'), 0, 0, tiled=True)  13.5 us
    all_to_all x1, blocking collectives, per_device(): part = lax.all_to_all(part, 'y', 0, 0, tiled=True).astype(f32)  12 us
    ppermute x3, starting transfers between devices, per_device(): moved = lax.ppermute(moved, 'y', step(y, k))  11.5 us
    ppermute x3, starting transfers between devices, per_device(): near = [lax.ppermute(hidden, 'zl', flip(zl, k)) for k in (1, 2, 3)]  11.4 us
    all_to_all x1, waiting for transfers between devices, per_device(): arrived = lax.all_to_all(slots, 'x', 0, 0, tiled=True)  10.3 us
    ppermute x3, starting transfers between devices, per_device(): distant = [lax.ppermute(other, 'zl', flip(zl, k)) for k in (1, 2, 3)]  10.1 us
    all_to_all x1, starting transfers between devices, per_device(): result = lax.all_to_all(result, ('zh', 'zl'), 0, 0, tiled=True)  9.58 us
  transfers between devices with their start and end apart: 21, of which 9 were waited for; matrix products, arithmetic and copies ran while one was open for 9% of the time, Pallas kernels for 3%

profile of v6, /device:TPU:32, one launch (start us, length us, event | category | flops | bytes accessed | tf_op | source)
XLA Modules:
  0.0 179.6 jit_solution(2122782558146277072)
XLA Ops:
  1.7 15.2 %all-to-all-start = ((bf16[16,16,896]{2,1,0:T(8,128)(2,1)}), bf16[16,16,896]{2,1,0:T(8,128)(2,1)S(1)}, u32[]{:S(2)}, u32[]{:S(2)}) async-start(bf16[16,16,896]{2,1,0:T(8,128)(2,1)} %get-tuple-element.18), calls=%async_computation | async-start | bytes 917504 | tf_op jit(solution)/shard_map/all_to_all | solution.py:166
  17.2 2.5 %dealt.1 = (bf16[4,96,2048]{2,1,0:T(8,128)(2,1)S(1)}, bf16[96,2048]{1,0:T(8,128)(2,1)}, bf16[96,2048]{1,0:T(8,128)(2,1)}, bf16[96,2048]{1,0:T(8,128)(2,1)}) fusion(bf16[4,96,2048]{2,1,0:T(8,128)(2,1)S(1)} %broadcast_in_dim.12, s32[]{:T(128)S(6)} %select_n.147, s32[2]{0:T(128)S(1)} %pad_add_fusion, bf16[1,96,8192]{2,1,0:T(8,128)(2,1)} %param.11), kind=kCustom, calls=%fused_computation.35 | custom fusion | bytes 3146244 | tf_op jit(solution)/shard_map/dealt/pallas_call | solution.py:66
  19.7 3.5 %collective-permute-start = (bf16[96,2048]{1,0:T(8,128)(2,1)}, bf16[96,2048]{1,0:T(8,128)(2,1)S(1)}, u32[]{:S(2)}, u32[]{:S(2)}) collective-permute-start(bf16[96,2048]{1,0:T(8,128)(2,1)} %get-tuple-element.34), channel_id=1, source_target_pairs={{0,16},{16,32},{32,48},{48,0},{1,17},{17,33},{33,49},{49,1},{2,18}... | collective-permute-start | bytes 1179656 | tf_op jit(solution)/shard_map/ppermute | solution.py:162
  23.2 4.8 %collective-permute-start.1 = (bf16[96,2048]{1,0:T(8,128)(2,1)}, bf16[96,2048]{1,0:T(8,128)(2,1)S(1)}, u32[]{:S(2)}, u32[]{:S(2)}) collective-permute-start(bf16[96,2048]{1,0:T(8,128)(2,1)} %get-tuple-element.36), channel_id=1, source_target_pairs={{0,32},{16,48},{32,0},{48,16},{1,33},{17,49},{33,1},{49,17},{2,34}... | collective-permute-start | bytes 1179656 | tf_op jit(solution)/shard_map/ppermute | solution.py:162
  28.0 3.3 %collective-permute-start.2 = (bf16[96,2048]{1,0:T(8,128)(2,1)}, bf16[96,2048]{1,0:T(8,128)(2,1)S(1)}, u32[]{:S(2)}, u32[]{:S(2)}) collective-permute-start(bf16[96,2048]{1,0:T(8,128)(2,1)} %get-tuple-element.38), channel_id=1, source_target_pairs={{0,48},{16,0},{32,16},{48,32},{1,49},{17,1},{33,17},{49,33},{2,50}... | collective-permute-start | bytes 1179656 | tf_op jit(solution)/shard_map/ppermute | solution.py:162
  36.0 5.1 %all-to-all-done = bf16[16,16,896]{2,1,0:T(8,128)(2,1)S(1)} async-done(((bf16[16,16,896]{2,1,0:T(8,128)(2,1)}), bf16[16,16,896]{2,1,0:T(8,128)(2,1)S(1)}, u32[]{:S(2)}, u32[]{:S(2)}) %all-to-all-start) | async-done | bytes 458784 | tf_op jit(solution)/shard_map/all_to_all | solution.py:166
  42.8 4.3 %all-to-all-start.1 = ((bf16[4,128,768]{2,1,0:T(8,128)(2,1)}), bf16[4,128,768]{2,1,0:T(8,128)(2,1)S(1)}, u32[]{:S(2)}, u32[]{:S(2)}) async-start(bf16[4,128,768]{2,1,0:T(8,128)(2,1)} %pad_maximum_fusion.1), calls=%async_computation.1 | async-start | bytes 1572864 | tf_op jit(solution)/shard_map/all_to_all | solution.py:192
  47.2 10.3 %all-to-all-done.1 = bf16[4,128,768]{2,1,0:T(8,128)(2,1)S(1)} async-done(((bf16[4,128,768]{2,1,0:T(8,128)(2,1)}), bf16[4,128,768]{2,1,0:T(8,128)(2,1)S(1)}, u32[]{:S(2)}, u32[]{:S(2)}) %all-to-all-start.1) | async-done | bytes 786464 | tf_op jit(solution)/shard_map/all_to_all | solution.py:192
  58.3 3.5 %collective-permute-start.5 = (bf16[64,6144]{1,0:T(8,128)(2,1)S(1)}, bf16[64,6144]{1,0:T(8,128)(2,1)S(1)}, u32[]{:S(2)}, u32[]{:S(2)}) collective-permute-start(bf16[64,6144]{1,0:T(8,128)(2,1)S(1)} %get-tuple-element.43), channel_id=1, source_target_pairs={{0,16},{16,32},{32,48},{48,0},{1,17},{17,33},{33,49},{49,1},{2,18}... | collective-permute-start | bytes 2359304 | tf_op jit(solution)/shard_map/ppermute | solution.py:201
  61.8 3.6 %collective-permute-start.6 = (bf16[64,6144]{1,0:T(8,128)(2,1)S(1)}, bf16[64,6144]{1,0:T(8,128)(2,1)S(1)}, u32[]{:S(2)}, u32[]{:S(2)}) collective-permute-start(bf16[64,6144]{1,0:T(8,128)(2,1)S(1)} %get-tuple-element.43), channel_id=1, source_target_pairs={{0,48},{16,0},{32,16},{48,32},{1,49},{17,1},{33,17},{49,33},{2,50}... | collective-permute-start | bytes 2359304 | tf_op jit(solution)/shard_map/ppermute | solution.py:202
  71.9 5.5 %collective-permute-done.5 = bf16[64,6144]{1,0:T(8,128)(2,1)S(1)} collective-permute-done((bf16[64,6144]{1,0:T(8,128)(2,1)S(1)}, bf16[64,6144]{1,0:T(8,128)(2,1)S(1)}, u32[]{:S(2)}, u32[]{:S(2)}) %collective-permute-start.5) | collective-permute-done | bytes 786464 | tf_op jit(solution)/shard_map/ppermute | solution.py:201
  79.7 4.8 %collective-permute-start.8 = (bf16[32,6144]{1,0:T(8,128)(2,1)S(1)}, bf16[32,6144]{1,0:T(8,128)(2,1)S(1)}, u32[]{:S(2)}, u32[]{:S(2)}) collective-permute-start(bf16[32,6144]{1,0:T(8,128)(2,1)S(1)} %slice.152), channel_id=1, source_target_pairs={{0,48},{16,0},{32,16},{48,32},{1,49},{17,1},{33,17},{49,33},{2,50}... | collective-permute-start | bytes 1179656 | tf_op jit(solution)/shard_map/ppermute | solution.py:205
  90.6 5.4 %gated.1 = bf16[256,256]{1,0:T(8,128)(2,1)} custom-call(s32[1]{0:T(128)} %bitcast.core_ref, bf16[256,6144]{1,0:T(8,128)(2,1)} %constant_dynamic-update-slice_fusion.rows_ref, bf16[6144,128]{1,0:T(8,128)(2,1)} %bitcast.119, bf16[6144,128]{1,0:T(8,128)(2,1)} %bitcast.121, bf16[6144,128]{1,0:T(8,128)(2,1)} %collective-permute-done.3.g1, ...), custom_call_target="tpu_custom_call" | custom-call | flops 1610612736 | bytes 9437184 | tf_op jit(solution)/shard_map/gated/pallas_call | solution.py:117
  96.1 8.5 %collective-permute-start.13 = (bf16[256,256]{1,0:T(8,128)(2,1)}, bf16[256,256]{1,0:T(8,128)(2,1)S(1)}, u32[]{:S(2)}, u32[]{:S(2)}) collective-permute-start(bf16[256,256]{1,0:T(8,128)(2,1)} %gated.1), channel_id=1, source_target_pairs={{0,256},{64,320},{128,384},{192,448},{256,0},{320,64},{384,128},{4... | collective-permute-start | bytes 393224 | tf_op jit(solution)/shard_map/ppermute | solution.py:224
  106.5 6.1 %collective-permute-start.11 = (bf16[256,256]{1,0:T(8,128)(2,1)}, bf16[256,256]{1,0:T(8,128)(2,1)S(1)}, u32[]{:S(2)}, u32[]{:S(2)}) collective-permute-start(bf16[256,256]{1,0:T(8,128)(2,1)} %gated.1), channel_id=1, source_target_pairs={{0,128},{64,192},{128,0},{192,64},{256,384},{320,448},{384,256},{4... | collective-permute-start | bytes 393224 | tf_op jit(solution)/shard_map/ppermute | solution.py:225
  112.7 3.4 %collective-permute-start.10 = (bf16[256,256]{1,0:T(8,128)(2,1)}, bf16[256,256]{1,0:T(8,128)(2,1)S(1)}, u32[]{:S(2)}, u32[]{:S(2)}) collective-permute-start(bf16[256,256]{1,0:T(8,128)(2,1)} %gated.1), channel_id=1, source_target_pairs={{0,64},{64,0},{128,192},{192,128},{256,320},{320,256},{384,448},{4... | collective-permute-start | bytes 393224 | tf_op jit(solution)/shard_map/ppermute | solution.py:225
  116.1 3.4 %collective-permute-start.16 = (bf16[256,256]{1,0:T(8,128)(2,1)S(1)}, bf16[256,256]{1,0:T(8,128)(2,1)S(1)}, u32[]{:S(2)}, u32[]{:S(2)}) collective-permute-start(bf16[256,256]{1,0:T(8,128)(2,1)S(1)} %collective-permute-done.13), channel_id=1, source_target_pairs={{0,192},{64,128},{128,64},{192,0},{256,448},{320,384},{384,320},{4... | collective-permute-start | bytes 393224 | tf_op jit(solution)/shard_map/ppermute | solution.py:226
  119.5 3.4 %collective-permute-start.15 = (bf16[256,256]{1,0:T(8,128)(2,1)S(1)}, bf16[256,256]{1,0:T(8,128)(2,1)S(1)}, u32[]{:S(2)}, u32[]{:S(2)}) collective-permute-start(bf16[256,256]{1,0:T(8,128)(2,1)S(1)} %collective-permute-done.13), channel_id=1, source_target_pairs={{0,128},{64,192},{128,0},{192,64},{256,384},{320,448},{384,256},{4... | collective-permute-start | bytes 393224 | tf_op jit(solution)/shard_map/ppermute | solution.py:226
  125.1 3.4 %collective-permute-start.14 = (bf16[256,256]{1,0:T(8,128)(2,1)S(1)}, bf16[256,256]{1,0:T(8,128)(2,1)S(1)}, u32[]{:S(2)}, u32[]{:S(2)}) collective-permute-start(bf16[256,256]{1,0:T(8,128)(2,1)S(1)} %collective-permute-done.13), channel_id=1, source_target_pairs={{0,64},{64,0},{128,192},{192,128},{256,320},{320,256},{384,448},{4... | collective-permute-start | bytes 393224 | tf_op jit(solution)/shard_map/ppermute | solution.py:226
  132.6 12.0 %all_to_all.25 = bf16[4,64,768]{2,1,0:T(8,128)(2,1)S(1)} all-to-all(bf16[4,64,768]{2,1,0:T(8,128)(2,1)S(1)} %constant_dynamic-slice_fusion), channel_id=1, replica_groups=mesh['zl'=8,'y'=4,'c'=2,'zh'=2,'x'=4] {'y'}, dimensions={0} | all-to-all | bytes 786432 | tf_op jit(solution)/shard_map/all_to_all | solution.py:240
  145.5 9.6 %all-to-all-start.3 = ((bf16[16,8,768]{2,1,0:T(8,128)(2,1)}), bf16[16,8,768]{2,1,0:T(8,128)(2,1)S(1)}, u32[]{:S(2)}, u32[]{:S(2)}) async-start(bf16[16,8,768]{2,1,0:T(8,128)(2,1)} %bitcast.42), calls=%async_computation.3 | async-start | bytes 393216 | tf_op jit(solution)/shard_map/all_to_all | solution.py:246
  155.1 13.5 %all-to-all-done.3 = bf16[16,8,768]{2,1,0:T(8,128)(2,1)S(1)} async-done(((bf16[16,8,768]{2,1,0:T(8,128)(2,1)}), bf16[16,8,768]{2,1,0:T(8,128)(2,1)S(1)}, u32[]{:S(2)}, u32[]{:S(2)}) %all-to-all-start.3) | async-done | bytes 196640 | tf_op jit(solution)/shard_map/all_to_all | solution.py:246
  169.3 3.3 %all-to-all-start.4 = ((bf16[4,16,768]{2,1,0:T(8,128)(2,1)}), bf16[4,16,768]{2,1,0:T(8,128)(2,1)S(1)}, u32[]{:S(2)}, u32[]{:S(2)}) async-start(bf16[4,16,768]{2,1,0:T(8,128)(2,1)} %pad_maximum_fusion.2), calls=%async_computation.4 | async-start | bytes 196608 | tf_op jit(solution)/shard_map/all_to_all | solution.py:250
  172.6 5.8 %all-to-all-done.4 = bf16[4,16,768]{2,1,0:T(8,128)(2,1)S(1)} async-done(((bf16[4,16,768]{2,1,0:T(8,128)(2,1)}), bf16[4,16,768]{2,1,0:T(8,128)(2,1)S(1)}, u32[]{:S(2)}, u32[]{:S(2)}) %all-to-all-start.4) | async-done | bytes 98336 | tf_op jit(solution)/shard_map/all_to_all | solution.py:250
  (97 shorter events, 34.7 us)
Async XLA Ops:
  1.7 39.3 %all-to-all-start = ((bf16[16,16,896]{2,1,0:T(8,128)(2,1)}), bf16[16,16,896]{2,1,0:T(8,128)(2,1)S(1)}, u32[]{:S(2)}, u32[]{:S(2)}) async-start(bf16[16,16,896]{2,1,0:T(8,128)(2,1)} %get-tuple-element.18), calls=%async_computation | async-start | bytes 917504 | tf_op jit(solution)/shard_map/all_to_all | solution.py:166
  19.7 16.2 %collective-permute-start = (bf16[96,2048]{1,0:T(8,128)(2,1)}, bf16[96,2048]{1,0:T(8,128)(2,1)S(1)}, u32[]{:S(2)}, u32[]{:S(2)}) collective-permute-start(bf16[96,2048]{1,0:T(8,128)(2,1)} %get-tuple-element.34), channel_id=1, source_target_pairs={{0,16},{16,32},{32,48},{48,0},{1,17},{17,33},{33,49},{49,1},{2,18}... | collective-permute-start | bytes 1179656 | tf_op jit(solution)/shard_map/ppermute | solution.py:162
  23.2 23.9 %collective-permute-start.1 = (bf16[96,2048]{1,0:T(8,128)(2,1)}, bf16[96,2048]{1,0:T(8,128)(2,1)S(1)}, u32[]{:S(2)}, u32[]{:S(2)}) collective-permute-start(bf16[96,2048]{1,0:T(8,128)(2,1)} %get-tuple-element.36), channel_id=1, source_target_pairs={{0,32},{16,48},{32,0},{48,16},{1,33},{17,49},{33,1},{49,17},{2,34}... | collective-permute-start | bytes 1179656 | tf_op jit(solution)/shard_map/ppermute | solution.py:162
  28.0 19.1 %collective-permute-start.2 = (bf16[96,2048]{1,0:T(8,128)(2,1)}, bf16[96,2048]{1,0:T(8,128)(2,1)S(1)}, u32[]{:S(2)}, u32[]{:S(2)}) collective-permute-start(bf16[96,2048]{1,0:T(8,128)(2,1)} %get-tuple-element.38), channel_id=1, source_target_pairs={{0,48},{16,0},{32,16},{48,32},{1,49},{17,1},{33,17},{49,33},{2,50}... | collective-permute-start | bytes 1179656 | tf_op jit(solution)/shard_map/ppermute | solution.py:162
  31.3 15.9 %collective-permute-start.3 = (bf16[6144,128]{1,0:T(8,128)(2,1)}, bf16[6144,128]{1,0:T(8,128)(2,1)}, u32[]{:S(2)}, u32[]{:S(2)}) collective-permute-start(bf16[6144,128]{1,0:T(8,128)(2,1)} %bitcast.118), channel_id=1, source_target_pairs={{0,8},{8,0},{1,9},{9,1},{2,10},{10,2},{3,11},{11,3},{4,12},{12,4},... | collective-permute-start | bytes 4718600 | tf_op jit(solution)/shard_map/ppermute | solution.py:150
  33.2 14.0 %collective-permute-start.4 = (bf16[6144,128]{1,0:T(8,128)(2,1)}, bf16[6144,128]{1,0:T(8,128)(2,1)}, u32[]{:S(2)}, u32[]{:S(2)}) collective-permute-start(bf16[6144,128]{1,0:T(8,128)(2,1)} %bitcast.120), channel_id=1, source_target_pairs={{0,8},{8,0},{1,9},{9,1},{2,10},{10,2},{3,11},{11,3},{4,12},{12,4},... | collective-permute-start | bytes 4718600 | tf_op jit(solution)/shard_map/ppermute | solution.py:151
  42.8 14.7 %all-to-all-start.1 = ((bf16[4,128,768]{2,1,0:T(8,128)(2,1)}), bf16[4,128,768]{2,1,0:T(8,128)(2,1)S(1)}, u32[]{:S(2)}, u32[]{:S(2)}) async-start(bf16[4,128,768]{2,1,0:T(8,128)(2,1)} %pad_maximum_fusion.1), calls=%async_computation.1 | async-start | bytes 1572864 | tf_op jit(solution)/shard_map/all_to_all | solution.py:192
  58.3 19.2 %collective-permute-start.5 = (bf16[64,6144]{1,0:T(8,128)(2,1)S(1)}, bf16[64,6144]{1,0:T(8,128)(2,1)S(1)}, u32[]{:S(2)}, u32[]{:S(2)}) collective-permute-start(bf16[64,6144]{1,0:T(8,128)(2,1)S(1)} %get-tuple-element.43), channel_id=1, source_target_pairs={{0,16},{16,32},{32,48},{48,0},{1,17},{17,33},{33,49},{49,1},{2,18}... | collective-permute-start | bytes 2359304 | tf_op jit(solution)/shard_map/ppermute | solution.py:201
  61.8 17.9 %collective-permute-start.6 = (bf16[64,6144]{1,0:T(8,128)(2,1)S(1)}, bf16[64,6144]{1,0:T(8,128)(2,1)S(1)}, u32[]{:S(2)}, u32[]{:S(2)}) collective-permute-start(bf16[64,6144]{1,0:T(8,128)(2,1)S(1)} %get-tuple-element.43), channel_id=1, source_target_pairs={{0,48},{16,0},{32,16},{48,32},{1,49},{17,1},{33,17},{49,33},{2,50}... | collective-permute-start | bytes 2359304 | tf_op jit(solution)/shard_map/ppermute | solution.py:202
  68.0 51.5 %collective-permute-start.9 = (bf16[384,2048]{1,0:T(8,128)(2,1)S(1)}, bf16[384,2048]{1,0:T(8,128)(2,1)}, u32[]{:S(2)}, u32[]{:S(2)}) collective-permute-start(bf16[384,2048]{1,0:T(8,128)(2,1)S(1)} %bitcast.111), channel_id=1, source_target_pairs={{0,8},{8,0},{1,9},{9,1},{2,10},{10,2},{3,11},{11,3},{4,12},{12,4},... | collective-permute-start | bytes 4718600 | tf_op jit(solution)/shard_map/ppermute | solution.py:200
  77.5 10.9 %collective-permute-start.7 = (bf16[32,6144]{1,0:T(8,128)(2,1)S(1)}, bf16[32,6144]{1,0:T(8,128)(2,1)S(1)}, u32[]{:S(2)}, u32[]{:S(2)}) collective-permute-start(bf16[32,6144]{1,0:T(8,128)(2,1)S(1)} %slice.151), channel_id=1, source_target_pairs={{0,16},{16,32},{32,48},{48,0},{1,17},{17,33},{33,49},{49,1},{2,18}... | collective-permute-start | bytes 1179656 | tf_op jit(solution)/shard_map/ppermute | solution.py:204
  79.7 10.1 %collective-permute-start.8 = (bf16[32,6144]{1,0:T(8,128)(2,1)S(1)}, bf16[32,6144]{1,0:T(8,128)(2,1)S(1)}, u32[]{:S(2)}, u32[]{:S(2)}) collective-permute-start(bf16[32,6144]{1,0:T(8,128)(2,1)S(1)} %slice.152), channel_id=1, source_target_pairs={{0,48},{16,0},{32,16},{48,32},{1,49},{17,1},{33,17},{49,33},{2,50}... | collective-permute-start | bytes 1179656 | tf_op jit(solution)/shard_map/ppermute | solution.py:205
  96.1 20.0 %collective-permute-start.13 = (bf16[256,256]{1,0:T(8,128)(2,1)}, bf16[256,256]{1,0:T(8,128)(2,1)S(1)}, u32[]{:S(2)}, u32[]{:S(2)}) collective-permute-start(bf16[256,256]{1,0:T(8,128)(2,1)} %gated.1), channel_id=1, source_target_pairs={{0,256},{64,320},{128,384},{192,448},{256,0},{320,64},{384,128},{4... | collective-permute-start | bytes 393224 | tf_op jit(solution)/shard_map/ppermute | solution.py:224
  104.6 20.5 %collective-permute-start.12 = (bf16[256,256]{1,0:T(8,128)(2,1)}, bf16[256,256]{1,0:T(8,128)(2,1)S(1)}, u32[]{:S(2)}, u32[]{:S(2)}) collective-permute-start(bf16[256,256]{1,0:T(8,128)(2,1)} %gated.1), channel_id=1, source_target_pairs={{0,192},{64,128},{128,64},{192,0},{256,448},{320,384},{384,320},{4... | collective-permute-start | bytes 393224 | tf_op jit(solution)/shard_map/ppermute | solution.py:225
  106.5 22.2 %collective-permute-start.11 = (bf16[256,256]{1,0:T(8,128)(2,1)}, bf16[256,256]{1,0:T(8,128)(2,1)S(1)}, u32[]{:S(2)}, u32[]{:S(2)}) collective-permute-start(bf16[256,256]{1,0:T(8,128)(2,1)} %gated.1), channel_id=1, source_target_pairs={{0,128},{64,192},{128,0},{192,64},{256,384},{320,448},{384,256},{4... | collective-permute-start | bytes 393224 | tf_op jit(solution)/shard_map/ppermute | solution.py:225
  112.7 16.4 %collective-permute-start.10 = (bf16[256,256]{1,0:T(8,128)(2,1)}, bf16[256,256]{1,0:T(8,128)(2,1)S(1)}, u32[]{:S(2)}, u32[]{:S(2)}) collective-permute-start(bf16[256,256]{1,0:T(8,128)(2,1)} %gated.1), channel_id=1, source_target_pairs={{0,64},{64,0},{128,192},{192,128},{256,320},{320,256},{384,448},{4... | collective-permute-start | bytes 393224 | tf_op jit(solution)/shard_map/ppermute | solution.py:225
  116.1 14.1 %collective-permute-start.16 = (bf16[256,256]{1,0:T(8,128)(2,1)S(1)}, bf16[256,256]{1,0:T(8,128)(2,1)S(1)}, u32[]{:S(2)}, u32[]{:S(2)}) collective-permute-start(bf16[256,256]{1,0:T(8,128)(2,1)S(1)} %collective-permute-done.13), channel_id=1, source_target_pairs={{0,192},{64,128},{128,64},{192,0},{256,448},{320,384},{384,320},{4... | collective-permute-start | bytes 393224 | tf_op jit(solution)/shard_map/ppermute | solution.py:226
  119.5 11.1 %collective-permute-start.15 = (bf16[256,256]{1,0:T(8,128)(2,1)S(1)}, bf16[256,256]{1,0:T(8,128)(2,1)S(1)}, u32[]{:S(2)}, u32[]{:S(2)}) collective-permute-start(bf16[256,256]{1,0:T(8,128)(2,1)S(1)} %collective-permute-done.13), channel_id=1, source_target_pairs={{0,128},{64,192},{128,0},{192,64},{256,384},{320,448},{384,256},{4... | collective-permute-start | bytes 393224 | tf_op jit(solution)/shard_map/ppermute | solution.py:226
  124.7 4.6 %copy-start = (bf16[256,256]{1,0:T(8,128)(2,1)S(1)}, bf16[256,256]{1,0:T(8,128)(2,1)}, u32[]{:S(2)}) copy-start(bf16[256,256]{1,0:T(8,128)(2,1)} %gated.1) | copy-start | bytes 393220
  125.1 7.0 %collective-permute-start.14 = (bf16[256,256]{1,0:T(8,128)(2,1)S(1)}, bf16[256,256]{1,0:T(8,128)(2,1)S(1)}, u32[]{:S(2)}, u32[]{:S(2)}) collective-permute-start(bf16[256,256]{1,0:T(8,128)(2,1)S(1)} %collective-permute-done.13), channel_id=1, source_target_pairs={{0,64},{64,0},{128,192},{192,128},{256,320},{320,256},{384,448},{4... | collective-permute-start | bytes 393224 | tf_op jit(solution)/shard_map/ppermute | solution.py:226
  132.5 45.9 %copy-start.2 = (f32[16,2]{0,1:T(2,128)S(1)}, f32[16,2]{0,1:T(2,128)}, u32[]{:S(2)}) copy-start(f32[16,2]{0,1:T(2,128)} %param.8) | copy-start | bytes 388
  132.5 45.9 %copy-start.1 = (s32[16,128]{1,0:T(8,128)S(1)}, s32[16,128]{1,0:T(8,128)}, u32[]{:S(2)}) copy-start(s32[16,128]{1,0:T(8,128)} %get-tuple-element.29) | copy-start | bytes 24580
  145.5 23.1 %all-to-all-start.3 = ((bf16[16,8,768]{2,1,0:T(8,128)(2,1)}), bf16[16,8,768]{2,1,0:T(8,128)(2,1)S(1)}, u32[]{:S(2)}, u32[]{:S(2)}) async-start(bf16[16,8,768]{2,1,0:T(8,128)(2,1)} %bitcast.42), calls=%async_computation.3 | async-start | bytes 393216 | tf_op jit(solution)/shard_map/all_to_all | solution.py:246
  169.3 9.1 %all-to-all-start.4 = ((bf16[4,16,768]{2,1,0:T(8,128)(2,1)}), bf16[4,16,768]{2,1,0:T(8,128)(2,1)S(1)}, u32[]{:S(2)}, u32[]{:S(2)}) async-start(bf16[4,16,768]{2,1,0:T(8,128)(2,1)} %pad_maximum_fusion.2), calls=%async_computation.4 | async-start | bytes 196608 | tf_op jit(solution)/shard_map/all_to_all | solution.py:250
